TPU v7x, 32 devices: a whole 2x2x4 slice. The times are simulated.
32 devices in a mesh: band: 16 (over z, y, core), ga: 2 (over x).
Axes of the slice: x: 2, y: 2, z: 4, core: 2. Of those that a mesh axis runs over, the one named last changes fastest.
Arguments:
- orbitals: bfloat16 [2, 16, 160, 128], P(None, 'band', 'ga'), may hold values from -8 to 8, as said below
- potential: float32 [480, 480], P('ga'), may hold values from -2 to 2
- slot_sticks: int32 [160], replicated, may hold values from -1 to 126, as said below
- stick_entries: int32 [160, 128], replicated, may hold values from -1 to 126, as said below
Outputs:
- applied_orbitals: bfloat16 [2, 16, 160, 128], P(None, 'band', 'ga')
- correlation: float32 [2, 16, 16], replicated
- reduced_hamiltonian: float32 [2, 16, 16], replicated
Inputs may be any that keep to these rules, and one draw needn't show every extreme that they name: `slot_sticks`: every gx with |gx| < 64 is held by exactly one slot; the other slots hold -1. Slots t with t // 80 = d are those of index d of ga; on some index of ga all 80 slots hold sticks. `stick_entries`: row t lists, in some order, gz + 63 for every gz with gx^2 + gz^2 < 64^2, gx being the stick of slot t, then -1 to the end of the row; rows of empty slots are all -1. `orbitals`: entries where stick_entries is -1 carry values that are not used.
All inputs are finite; a program needn't handle non-finite values.
Results may differ from a plain program's by a relative error of at most 0.001.
Values may be sent and summed in bfloat16 or wider, within the bound.
No kernel may reach another device: no remote copies, remote signals or barrier semaphores. Data moves between devices by JAX's collectives and lax.ppermute only.
A program may use at most 64 MiB of HBM per device.

v0:
```python
import math

import jax
import jax.numpy as jnp
import numpy as np
from jax import lax
from jax.experimental import pallas as pl
from jax.experimental.pallas import tpu as pltpu
from jax.sharding import PartitionSpec as P


F32 = jnp.float32
BF16 = jnp.bfloat16
VMEM_SPEC = pl.BlockSpec(memory_space=pltpu.VMEM)
SMEM_SPEC = pl.BlockSpec(memory_space=pltpu.SMEM)
FIRST_FLOPS = 3_000_000_000
SPREAD_FLOPS = 1_500_000_000
GRID_FLOPS = 3_000_000_000
KERNEL_PARAMS = pltpu.CompilerParams(vmem_limit_bytes=16 * 1024 * 1024)


def hi_lo_table(values):
    high = jnp.asarray(values, F32).astype(BF16)
    high_np = np.asarray(values, np.float32).astype(jnp.bfloat16)
    low_np = (values - high_np.astype(np.float64)).astype(jnp.bfloat16)
    return high_np, low_np


def twiddle_tables(points, radius, group_count):
    width = 2 * radius
    planes = points // group_count
    z = np.arange(points, dtype=np.int64)
    gz = np.arange(width, dtype=np.int64) - radius + 1
    angle_z = (z[:, None] * gz[None, :] % points) * (2.0 * np.pi / points)
    forward = np.concatenate([np.cos(angle_z), np.sin(angle_z)], axis=1)
    forward = forward.reshape(group_count, planes, 2 * width)
    backward = np.ascontiguousarray(np.transpose(forward, (0, 2, 1)))
    gx = np.arange(radius, dtype=np.int64)
    angle_x = (gx[:, None] * z[None, :] % points) * (2.0 * np.pi / points)
    x_table = np.concatenate([np.cos(angle_x), np.sin(angle_x)], axis=0)
    z_high, z_low = hi_lo_table(forward)
    zt_high, zt_low = hi_lo_table(backward)
    x_high, x_low = hi_lo_table(x_table)
    xt = np.concatenate([x_high.T, x_low.T], axis=1)
    return z_high, z_low, zt_high, zt_low, x_high, x_low, xt


def split(values):
    high = values.astype(BF16)
    low = (values - high.astype(F32)).astype(BF16)
    return high, low


def dot(left, right):
    return jnp.dot(left, right, preferred_element_type=F32)


def canonical_lane(sticks, radius):
    gx = sticks - radius + 1
    return jnp.where(gx >= 0, gx, radius - gx)


def rows_kernel(out_ref):
    out_ref[...] = lax.broadcasted_iota(jnp.int32, out_ref.shape, 0).astype(F32)


def sticks_of(sticks_ref, group, slots):
    sticks = sticks_ref[...]
    row = sticks[:, :slots]
    for index in range(1, sticks.shape[1] // slots):
        row = jnp.where(group == index, sticks[:, index * slots : (index + 1) * slots], row)
    return row


def spread_kernel(ga_ref, rows_ref, orbitals_ref, entries_ref, sticks_ref, out_ref, e_ref, re_ref, im_ref):
    width = entries_ref.shape[2]
    radius = width // 2
    slots = entries_ref.shape[1]
    ga = ga_ref[0]
    e_ref[...] = entries_ref[ga].astype(F32).T
    re_ref[...] = orbitals_ref[0, 0].astype(F32).T
    im_ref[...] = orbitals_ref[1, 0].astype(F32).T
    position = rows_ref[...]

    def step(k, carry):
        real_part, imag_part = carry
        match = e_ref[pl.ds(k, 1), :] == position
        real_part = jnp.where(match, re_ref[pl.ds(k, 1), :], real_part)
        imag_part = jnp.where(match, im_ref[pl.ds(k, 1), :], imag_part)
        return real_part, imag_part

    zeros = jnp.zeros((width, slots), F32)
    real_part, imag_part = lax.fori_loop(0, width, step, (zeros, zeros), unroll=4)
    spread = jnp.concatenate([real_part, imag_part], axis=0).astype(BF16)
    lane = canonical_lane(sticks_of(sticks_ref, ga, slots), radius)
    choose = (lax.broadcasted_iota(jnp.int32, (width, slots), 0) == lane).astype(F32).astype(BF16)
    out_ref[...] = lax.dot_general(
        spread, choose, (((1,), (1,)), ((), ())), preferred_element_type=F32
    ).astype(BF16)


def grid_kernel(ga_ref, coeffs_refs, potential_ref, sticks_ref, tables, own_ref, send_ref):
    z_high, z_low, zt_high, zt_low, x_high, x_low, xt = tables
    planes, _ = potential_ref.shape
    width = coeffs_refs[0].shape[1]
    radius = width // 2
    slots = own_ref.shape[0]
    groups = sticks_ref.shape[1] // slots
    ga = ga_ref[0]
    coeffs = coeffs_refs[0][...].astype(F32)
    for ref in coeffs_refs[1:]:
        coeffs = coeffs + ref[...].astype(F32)
    real_part, imag_part = coeffs[:width], coeffs[width:]
    rows = jnp.concatenate(
        [
            jnp.concatenate([real_part, imag_part], axis=1),
            jnp.concatenate([-imag_part, real_part], axis=1),
        ],
        axis=0,
    ).astype(BF16)
    columns = dot(z_high[ga], rows) + dot(z_low[ga], rows)
    col_re, col_im = columns[:, :width], columns[:, width:]
    rol_re, rol_im = pltpu.roll(col_re, radius, 1), pltpu.roll(col_im, radius, 1)
    even = lax.broadcasted_iota(jnp.int32, (planes, width), 1) < radius
    parity = jnp.concatenate(
        [
            jnp.where(even, col_re + rol_re, col_im - rol_im),
            jnp.where(even, col_im + rol_im, rol_re - col_re),
        ],
        axis=0,
    )
    par_high, par_low = split(parity)
    table = x_high[...]
    field = dot(jnp.concatenate([par_high, par_low], axis=1), jnp.concatenate([table, table], axis=0))
    field = field + dot(par_high, x_low[...])
    values = potential_ref[...]
    product = jnp.concatenate([values, values], axis=0) * field
    prod_high, prod_low = split(product)
    table_t = xt[...]
    wide = dot(prod_high, table_t)
    back = wide[:, :width] + wide[:, width:] + dot(prod_low, table_t[:, :width])
    back_re, back_im = back[:planes], back[planes:]
    rol_re, rol_im = pltpu.roll(back_re, radius, 1), pltpu.roll(back_im, radius, 1)
    gathered = jnp.concatenate(
        [
            jnp.where(even, back_re + rol_im, rol_re - back_im),
            jnp.where(even, back_im - rol_re, rol_im + back_re),
        ],
        axis=1,
    )
    gat_high, gat_low = split(gathered)
    spectra = dot(zt_high[ga], gat_high) + dot(zt_low[ga], gat_high) + dot(zt_high[ga], gat_low)
    spectra = jnp.concatenate(
        [
            spectra[:width, :width] + spectra[width:, width:],
            spectra[:width, width:] - spectra[width:, :width],
        ],
        axis=0,
    )
    spec_high, spec_low = split(spectra)
    spec = jnp.concatenate([spec_high, spec_low], axis=1)
    lanes = lax.broadcasted_iota(jnp.int32, (slots, width), 1)
    for distance in range(groups):
        group = lax.rem(ga + distance, groups)
        lane_row = canonical_lane(sticks_of(sticks_ref, group, slots), radius).astype(F32)
        lane_col = jnp.broadcast_to(lane_row, (width, slots)).T.astype(jnp.int32)
        choose = (lane_col == lanes).astype(F32).astype(BF16)
        picked = lax.dot_general(
            jnp.concatenate([choose, choose], axis=1), spec, (((1,), (1,)), ((), ())), preferred_element_type=F32
        )
        if distance == 0:
            own_ref[...] = picked
        else:
            send_ref[distance - 1] = picked


def apply_part(ga, partial_refs, orbitals_ref, entries_ref, sticks_ref, points):
    width = entries_ref.shape[2]
    radius = width // 2
    total = partial_refs[0][...]
    for ref in partial_refs[1:]:
        total = total + ref[...]
    entries = entries_ref[ga]
    present = entries >= 0
    index = jnp.maximum(entries, 0)
    gx_row = (sticks_of(sticks_ref, ga, entries.shape[0]) - radius + 1).astype(F32)
    gx = jnp.broadcast_to(gx_row, (width, gx_row.shape[1])).T
    gz = (entries - radius + 1).astype(F32)
    kinetic = (gx * gx + gz * gz) * (1.0 / (radius * radius))
    result = []
    for part in range(2):
        picked = jnp.take_along_axis(
            total[:, part * width : (part + 1) * width], index, axis=1, mode="promise_in_bounds"
        )
        value = kinetic * orbitals_ref[part, 0].astype(F32) + picked * (1.0 / (points * points))
        result.append(jnp.where(present, value, 0.0).astype(BF16))
    return result, present


def final_kernel(points, ga_ref, partial_refs, orbitals_ref, entries_ref, sticks_ref, psi_refs, out_ref, sums_ref):
    ga = ga_ref[0]
    result, present = apply_part(ga, partial_refs, orbitals_ref, entries_ref, sticks_ref, points)
    for part in range(2):
        out_ref[part, 0] = result[part]
    _, width = present.shape
    h_re, h_im = result[0].astype(F32), result[1].astype(F32)
    m_re = jnp.where(present, orbitals_ref[0, 0].astype(F32), 0.0)
    m_im = jnp.where(present, orbitals_ref[1, 0].astype(F32), 0.0)
    rows = [[], [], [], []]
    for psi_ref in psi_refs:
        for band in range(psi_ref.shape[1]):
            left_re = psi_ref[0, band].astype(F32)
            left_im = psi_ref[1, band].astype(F32)
            for place, (right_re, right_im) in enumerate(((m_re, m_im), (h_re, h_im))):
                rows[2 * place].append(jnp.sum(left_re * right_re + left_im * right_im, axis=0, keepdims=True))
                rows[2 * place + 1].append(jnp.sum(left_re * right_im - left_im * right_re, axis=0, keepdims=True))
    flat = sum(rows, [])
    lanes = sums_ref.shape[1]
    if len(flat) < lanes:
        flat.append(jnp.zeros((lanes - len(flat), width), F32))
    sums = jnp.sum(jnp.concatenate(flat, axis=0).T, axis=0, keepdims=True)
    sums_ref[...] = jnp.broadcast_to(sums, sums_ref.shape)


def assemble_kernel(groups, inner, blocks, scale, sums_ref, corr_ref, ham_ref):
    bands = inner * blocks
    shifts = blocks // 2 + 1
    count = shifts * inner
    total = sums_ref[0:bands, :]
    for group in range(1, groups):
        total = total + sums_ref[group * bands : (group + 1) * bands, :]
    lanes = total.shape[1]
    total = jnp.concatenate([total, jnp.zeros((lanes - bands, lanes), F32)], axis=0).T * scale
    row = lax.broadcasted_iota(jnp.int32, (lanes, lanes), 0)
    col = lax.broadcasted_iota(jnp.int32, (lanes, lanes), 1)
    row, col = row[:bands], col[:bands]
    shift_bits = int(math.log2(inner))
    row_block = lax.shift_right_logical(row, shift_bits)
    col_block = lax.shift_right_logical(col, shift_bits)
    away = row_block - col_block
    away = jnp.where(away < 0, away + blocks, away)
    slot = away * inner + lax.bitwise_xor(lax.bitwise_and(row, inner - 1), lax.bitwise_and(col, inner - 1))
    covered = away < shifts
    for place, ref in enumerate((corr_ref, ham_ref)):
        for part in range(2):
            base = (2 * place + part) * count
            direct = jnp.zeros((bands, lanes), F32)
            for index in range(count):
                direct = jnp.where(slot == index, total[base + index : base + index + 1, :], direct)
            padded = jnp.concatenate([direct, jnp.zeros((lanes - bands, lanes), F32)], axis=0)
            mirror = padded.T[:bands]
            if part:
                mirror = -mirror
            ref[part] = jnp.where(covered, direct, mirror)[:, :bands]


def general_matrices(psi, masked, applied, inner, blocks, scale):
    bands = inner * blocks
    shifts = blocks // 2 + 1
    count = shifts * inner
    left = jnp.concatenate(psi, axis=1).reshape(2, count, -1)
    right = jnp.stack([masked.reshape(2, -1), applied.reshape(2, -1)])
    product = jnp.einsum("cin,mdn->mcdi", left, right, preferred_element_type=F32)
    block = jnp.stack([product[:, 0, 0] + product[:, 1, 1], product[:, 0, 1] - product[:, 1, 0]], axis=1)
    everywhere = lax.all_gather(lax.psum(block * scale, "ga"), "band", axis=0)
    row, col = np.meshgrid(np.arange(bands), np.arange(bands), indexing="ij")
    away = (row // inner - col // inner) % blocks
    slot = np.where(away < shifts, away * inner + ((row % inner) ^ (col % inner)), 0)
    flat = jnp.transpose(everywhere, (1, 2, 0, 3)).reshape(4 * bands, count)
    index = jnp.asarray(np.tile(slot.T, (4, 1)), jnp.int32)
    direct = jnp.take_along_axis(flat, index, axis=1).reshape(2, 2, bands, bands)
    direct = jnp.swapaxes(direct, 2, 3)
    sign = jnp.asarray([1.0, -1.0], F32)[None, :, None, None]
    full = jnp.where(jnp.asarray(away < shifts), direct, sign * jnp.swapaxes(direct, 2, 3))
    return full[0], full[1]


def body(band_total, groups, orbitals, potential, slot_sticks, stick_entries):
    _, points = potential.shape
    width = stick_entries.shape[1]
    radius = width // 2
    slots = orbitals.shape[2]
    inner = math.gcd(band_total, 4)
    blocks = band_total // inner
    shifts = blocks // 2 + 1
    ga = lax.axis_index("ga").astype(jnp.int32).reshape(1)
    entries = stick_entries.reshape(groups, slots, width)
    sticks = slot_sticks.reshape(1, groups * slots)
    tables = [jnp.asarray(t) for t in twiddle_tables(points, radius, groups)]

    rows = pl.pallas_call(
        rows_kernel,
        out_shape=jax.ShapeDtypeStruct((width, slots), F32),
        out_specs=VMEM_SPEC,
        compiler_params=KERNEL_PARAMS,
        cost_estimate=pl.CostEstimate(flops=FIRST_FLOPS, bytes_accessed=0, transcendentals=0),
        name="rows",
    )()
    orbitals, rows = lax.optimization_barrier((orbitals, rows))
    near = [orbitals]
    for shift in range(1, shifts):
        pairs = [(i, (i - inner * shift) % band_total) for i in range(band_total)]
        near.append(lax.ppermute(orbitals, "band", pairs))

    place = pl.pallas_call(
        spread_kernel,
        out_shape=jax.ShapeDtypeStruct((2 * width, width), BF16),
        in_specs=[SMEM_SPEC] + [VMEM_SPEC] * 4,
        out_specs=VMEM_SPEC,
        scratch_shapes=[pltpu.VMEM((width, slots), F32)] * 3,
        compiler_params=KERNEL_PARAMS,
        cost_estimate=pl.CostEstimate(flops=SPREAD_FLOPS, bytes_accessed=0, transcendentals=0),
        name="spread",
    )
    coeffs = place(ga, rows, orbitals, entries, sticks)
    all_coeffs = [coeffs]
    for distance in range(1, groups):
        pairs = [(i, (i + distance) % groups) for i in range(groups)]
        all_coeffs.append(lax.ppermute(coeffs, "ga", pairs))

    received, *near = lax.optimization_barrier((all_coeffs[-1], *near))
    all_coeffs[-1] = received
    psi, order, step = [jnp.concatenate(near, axis=1)], [0], inner // 2

    def widen(parts, order, step):
        pairs = [(i, i ^ step) for i in range(band_total)]
        return parts + [lax.ppermute(part, "band", pairs) for part in parts], order + [o ^ step for o in order]

    while step > 1:
        psi, order = widen(psi, order, step)
        step //= 2

    def run_grid(ga_ref, *refs):
        count = len(all_coeffs)
        grid_kernel(ga_ref, refs[:count], refs[count], refs[count + 1], refs[count + 2 : count + 9], *refs[count + 9 :])

    own, send = pl.pallas_call(
        run_grid,
        out_shape=(
            jax.ShapeDtypeStruct((slots, 2 * width), F32),
            jax.ShapeDtypeStruct((groups - 1, slots, 2 * width), F32),
        ),
        in_specs=[SMEM_SPEC] + [VMEM_SPEC] * (len(all_coeffs) + 9),
        out_specs=(VMEM_SPEC, VMEM_SPEC),
        compiler_params=KERNEL_PARAMS,
        cost_estimate=pl.CostEstimate(flops=GRID_FLOPS, bytes_accessed=0, transcendentals=0),
        name="grid",
    )(ga, *all_coeffs, potential, sticks, *tables)
    own, *psi = lax.optimization_barrier((own, *psi))
    if step:
        psi, order = widen(psi, order, step)
    psi = [psi[order.index(q)] for q in range(inner)]
    partials = [own]
    for distance in range(1, groups):
        pairs = [(i, (i + distance) % groups) for i in range(groups)]
        partials.append(lax.ppermute(send[distance - 1], "ga", pairs))

    scale = 1.0 / (4.0 * radius * radius)
    out_type = jax.ShapeDtypeStruct(orbitals.shape, BF16)
    small = 4 * shifts * inner <= 128 and band_total <= 128
    count = len(partials)
    if not small:

        def run_apply(ga_ref, *refs):
            result, _ = apply_part(ga_ref[0], refs[:count], *refs[count : count + 3], points)
            refs[count + 3][0, 0] = result[0]
            refs[count + 3][1, 0] = result[1]

        applied = pl.pallas_call(
            run_apply,
            out_shape=out_type,
            in_specs=[SMEM_SPEC] + [VMEM_SPEC] * (count + 3),
            out_specs=VMEM_SPEC,
            compiler_params=KERNEL_PARAMS,
            name="apply",
        )(ga, *partials, orbitals, entries, sticks)
        own_lists = lax.dynamic_index_in_dim(entries, ga[0], 0, keepdims=False)
        masked = jnp.where(own_lists >= 0, orbitals, jnp.zeros_like(orbitals))
        left = [p for p in psi]
        left = [jnp.stack(left, axis=2).reshape(2, shifts * inner, slots, width)]
        correlation, reduced = general_matrices(left, masked, applied, inner, blocks, scale)
        return applied, correlation, reduced

    def run_final(ga_ref, *refs):
        rest = refs[count + 3 :]
        final_kernel(
            points, ga_ref, refs[:count], *refs[count : count + 3], [SplitBands(rest[:inner], s) for s in range(shifts)], *rest[inner:]
        )

    applied, sums = pl.pallas_call(
        run_final,
        out_shape=(out_type, jax.ShapeDtypeStruct((groups * band_total, 128), F32)),
        in_specs=[SMEM_SPEC] + [VMEM_SPEC] * (count + 3 + inner),
        out_specs=(VMEM_SPEC, VMEM_SPEC),
        compiler_params=KERNEL_PARAMS,
        name="final",
    )(ga, *partials, orbitals, entries, sticks, *psi)
    everywhere = lax.all_to_all(sums, ("ga", "band"), split_axis=0, concat_axis=0, tiled=True)
    matrix = jax.ShapeDtypeStruct((2, band_total, band_total), F32)

    def run_assemble(sums_ref, corr_ref, ham_ref):
        assemble_kernel(groups, inner, blocks, scale, sums_ref, corr_ref, ham_ref)

    correlation, reduced = pl.pallas_call(
        run_assemble,
        out_shape=(matrix, matrix),
        in_specs=[VMEM_SPEC],
        out_specs=(VMEM_SPEC, VMEM_SPEC),
        compiler_params=KERNEL_PARAMS,
        name="assemble",
    )(everywhere)
    return applied, correlation, reduced


class SplitBands:
    def __init__(self, refs, shift):
        self.refs = refs
        self.shift = shift
        self.shape = (2, len(refs))

    def __getitem__(self, key):
        part, band = key
        return self.refs[band][part, self.shift]


def solution(mesh):
    band_total = mesh.shape["band"]
    groups = mesh.shape["ga"]

    def mapped(orbitals, potential, slot_sticks, stick_entries):
        return body(band_total, groups, orbitals, potential, slot_sticks, stick_entries)

    return jax.shard_map(
        mapped,
        mesh=mesh,
        in_specs=(P(None, "band", "ga", None), P("ga", None), P(), P()),
        out_specs=(P(None, "band", "ga", None), P(), P()),
        check_vma=False,
    )
```

profile of v0, /device:TPU:0, one launch (start us, length us, event | category | flops | bytes accessed | tf_op | source)
XLA Modules:
  0.0 35.8 jit_solution(12965488258383839112)
XLA Ops:
  0.7 0.0 copy-start.2
  0.7 0.7 %copy-done = bf16[2,1,80,128]{3,2,1,0:T(8,128)(2,1)S(1)} copy-done((bf16[2,1,80,128]{3,2,1,0:T(8,128)(2,1)S(1)}, bf16[2,1,80,128]{3,2,1,0:T(8,128)(2,1)}, u32[]{:S(2)}) %copy-start) | copy-done | bytes 40984
  1.4 0.1 copy-done.1
  1.6 0.0 copy-start.6
  1.6 0.0 copy-start.7
  1.6 0.0 copy-start.8
  1.6 0.0 copy-start.10
  1.6 1.5 %spread.1.refs_0_ = bf16[256,128]{1,0:T(8,128)(2,1)S(1)} custom-call(s32[1]{0:T(128)} %bitcast.ga_ref, f32[128,80]{1,0:T(8,128)S(1)} %rows.1.rows_ref, bf16[2,1,80,128]{3,2,1,0:T(8,128)(2,1)S(1)} %copy-done, s32[2,80,128]{2,1,0:T(8,128)S(1)} %bitcast.8, s32[1,160]{1,0:T(1,128)S(1)} %bitcast.12), custom_call_target="tpu_custom_call" | custom-call | flops 1500000000 | tf_op jit(solution)/shard_map/spread/pallas_call | solution.py:315
  3.1 0.0 copy-start.9
  3.1 3.0 %collective-permute-start = (bf16[256,128]{1,0:T(8,128)(2,1)S(1)}, bf16[256,128]{1,0:T(8,128)(2,1)S(1)}, u32[]{:S(2)}, u32[]{:S(2)}) collective-permute-start(bf16[256,128]{1,0:T(8,128)(2,1)S(1)} %spread.1.refs_0_), channel_id=1, source_target_pairs={{0,1},{1,0},{2,3},{3,2},{4,5},{5,4},{6,7},{7,6},{8,9},{9,8},{10,11... | collective-permute-start | bytes 196616 | tf_op jit(solution)/shard_map/ppermute | solution.py:319
  6.2 2.6 %collective-permute-start.2 = (bf16[2,1,80,128]{3,2,1,0:T(8,128)(2,1)S(1)}, bf16[2,1,80,128]{3,2,1,0:T(8,128)(2,1)S(1)}, u32[]{:S(2)}, u32[]{:S(2)}) collective-permute-start(bf16[2,1,80,128]{3,2,1,0:T(8,128)(2,1)S(1)} %copy-done), channel_id=1, source_target_pairs={{0,16},{2,18},{4,20},{6,22},{8,24},{10,26},{12,28},{14,30},{16,0},... | collective-permute-start | bytes 122888 | tf_op jit(solution)/shard_map/ppermute | solution.py:303
  8.7 1.3 %collective-permute-start.1 = (bf16[2,1,80,128]{3,2,1,0:T(8,128)(2,1)S(1)}, bf16[2,1,80,128]{3,2,1,0:T(8,128)(2,1)S(1)}, u32[]{:S(2)}, u32[]{:S(2)}) collective-permute-start(bf16[2,1,80,128]{3,2,1,0:T(8,128)(2,1)S(1)} %copy-done), channel_id=1, source_target_pairs={{0,24},{2,26},{4,28},{6,30},{8,0},{10,2},{12,4},{14,6},{16,8},{18,... | collective-permute-start | bytes 122888 | tf_op jit(solution)/shard_map/ppermute | solution.py:303
  10.1 1.1 %collective-permute-done.2 = bf16[2,1,80,128]{3,2,1,0:T(8,128)(2,1)S(1)} collective-permute-done((bf16[2,1,80,128]{3,2,1,0:T(8,128)(2,1)S(1)}, bf16[2,1,80,128]{3,2,1,0:T(8,128)(2,1)S(1)}, u32[]{:S(2)}, u32[]{:S(2)}) %collective-permute-start.2) | collective-permute-done | bytes 40992 | tf_op jit(solution)/shard_map/ppermute | solution.py:303
  11.2 1.6 %collective-permute-done.1 = bf16[2,1,80,128]{3,2,1,0:T(8,128)(2,1)S(1)} collective-permute-done((bf16[2,1,80,128]{3,2,1,0:T(8,128)(2,1)S(1)}, bf16[2,1,80,128]{3,2,1,0:T(8,128)(2,1)S(1)}, u32[]{:S(2)}, u32[]{:S(2)}) %collective-permute-start.1) | collective-permute-done | bytes 40992 | tf_op jit(solution)/shard_map/ppermute | solution.py:303
  12.7 0.0 collective-permute-done.refs_1_
  12.8 1.6 %collective-permute-start.3 = (bf16[2,3,80,128]{3,2,1,0:T(8,128)(2,1)S(1)}, bf16[2,3,80,128]{3,2,1,0:T(8,128)(2,1)S(1)}, u32[]{:S(2)}, u32[]{:S(2)}) collective-permute-start(bf16[2,3,80,128]{3,2,1,0:T(8,128)(2,1)S(1)} %constant_dynamic-update-slice_fusion.refs_5_), channel_id=1, source_target_pairs={{0,4},{2,6},{4,0},{6,2},{8,12},{10,14},{12,8},{14,10},{16,20},{18,... | collective-permute-start | bytes 368648 | tf_op jit(solution)/shard_map/ppermute | solution.py:327
  14.4 1.8 %grid.1 = (f32[80,256]{1,0:T(8,128)S(1)}, f32[1,80,256]{2,1,0:T(8,128)S(1)}) custom-call(s32[1]{0:T(128)} %bitcast.ga_ref, bf16[256,128]{1,0:T(8,128)(2,1)S(1)} %spread.1.refs_0_, bf16[256,128]{1,0:T(8,128)(2,1)S(1)} %collective-permute-done.refs_1_, f32[240,480]{1,0:T(8,128)S(1)} %copy-done.3, s32[1,160]{1,0:T(1,128)S(1)} %bitcast.13, ...), custom_call_target="tpu_custom_call" | custom-call | flops 3000000000 | tf_op jit(solution)/shard_map/grid/pallas_call | solution.py:337
  16.2 1.5 %collective-permute-done.3.refs_7_ = bf16[2,3,80,128]{3,2,1,0:T(8,128)(2,1)S(1)} collective-permute-done((bf16[2,3,80,128]{3,2,1,0:T(8,128)(2,1)S(1)}, bf16[2,3,80,128]{3,2,1,0:T(8,128)(2,1)S(1)}, u32[]{:S(2)}, u32[]{:S(2)}) %collective-permute-start.3) | collective-permute-done | bytes 122912 | tf_op jit(solution)/shard_map/ppermute | solution.py:327
  17.7 0.5 %collective-permute-start.6 = (bf16[2,3,80,128]{3,2,1,0:T(8,128)(2,1)S(1)}, bf16[2,3,80,128]{3,2,1,0:T(8,128)(2,1)S(1)}, u32[]{:S(2)}, u32[]{:S(2)}) collective-permute-start(bf16[2,3,80,128]{3,2,1,0:T(8,128)(2,1)S(1)} %collective-permute-done.3.refs_7_), channel_id=1, source_target_pairs={{0,2},{2,0},{4,6},{6,4},{8,10},{10,8},{12,14},{14,12},{16,18},{18,... | collective-permute-start | bytes 368648 | tf_op jit(solution)/shard_map/ppermute | solution.py:327
  18.2 0.5 %collective-permute-start.4 = (f32[80,256]{1,0:T(8,128)S(1)}, f32[80,256]{1,0:T(8,128)S(1)}, u32[]{:S(2)}, u32[]{:S(2)}) collective-permute-start(f32[80,256]{1,0:T(8,128)S(1)} %bitcast.15), channel_id=1, source_target_pairs={{0,1},{1,0},{2,3},{3,2},{4,5},{5,4},{6,7},{7,6},{8,9},{9,8},{10,11... | collective-permute-start | bytes 245768 | tf_op jit(solution)/shard_map/ppermute | solution.py:356
  18.8 3.9 %collective-permute-done.4.refs_1_ = f32[80,256]{1,0:T(8,128)S(1)} collective-permute-done((f32[80,256]{1,0:T(8,128)S(1)}, f32[80,256]{1,0:T(8,128)S(1)}, u32[]{:S(2)}, u32[]{:S(2)}) %collective-permute-start.4) | collective-permute-done | bytes 81952 | tf_op jit(solution)/shard_map/ppermute | solution.py:356
  22.7 0.9 %final.1 = (bf16[2,1,80,128]{3,2,1,0:T(8,128)(2,1)}, f32[32,128]{1,0:T(8,128)S(1)}) custom-call(s32[1]{0:T(128)} %bitcast.ga_ref, f32[80,256]{1,0:T(8,128)S(1)} %get-tuple-element.25.refs_0_, f32[80,256]{1,0:T(8,128)S(1)} %collective-permute-done.4.refs_1_, bf16[2,1,80,128]{3,2,1,0:T(8,128)(2,1)S(1)} %copy-done, s32[2,80,128]{2,1,0:T(8,128)S(1)} %bitcast.9, ...), custom_call_target="tpu_custom_call" | custom-call | tf_op jit(solution)/shard_map/final/pallas_call | solution.py:390
  23.6 11.4 %all_to_all.11 = f32[32,1,128]{2,1,0:T(1,128)S(1)} all-to-all(f32[32,1,128]{2,1,0:T(1,128)S(1)} %bitcast.11), channel_id=1, replica_groups=mesh['band'=16,'ga'=2] {'ga','band'}, dimensions={0} | all-to-all | bytes 32768 | tf_op jit(solution)/shard_map/all_to_all | solution.py:398
  35.1 0.8 %assemble.1 = (f32[2,16,16]{2,1,0:T(8,128)}, f32[2,16,16]{2,1,0:T(8,128)}) custom-call(f32[32,128]{1,0:T(8,128)S(1)} %bitcast.10), custom_call_target="tpu_custom_call" | custom-call | tf_op jit(solution)/shard_map/assemble/pallas_call | solution.py:404
  (21 shorter events, 0.1 us)
Async XLA Ops:
  0.6 0.8 %copy-start = (bf16[2,1,80,128]{3,2,1,0:T(8,128)(2,1)S(1)}, bf16[2,1,80,128]{3,2,1,0:T(8,128)(2,1)}, u32[]{:S(2)}) copy-start(bf16[2,1,80,128]{3,2,1,0:T(8,128)(2,1)} %refs_2_.2) | copy-start | bytes 122884
  0.6 0.9 %copy-start.1 = (s32[160,128]{1,0:T(8,128)S(1)}, s32[160,128]{1,0:T(8,128)}, u32[]{:S(2)}) copy-start(s32[160,128]{1,0:T(8,128)} %param.14) | copy-start | bytes 245764
  0.7 0.9 %copy-start.2 = (s32[160]{0:T(256)S(1)}, s32[160]{0:T(256)}, u32[]{:S(2)}) copy-start(s32[160]{0:T(256)} %param.13) | copy-start | bytes 1924
  1.5 12.8 %copy-start.3 = (f32[240,480]{1,0:T(8,128)S(1)}, f32[240,480]{1,0:T(8,128)}, u32[]{:S(2)}) copy-start(f32[240,480]{1,0:T(8,128)} %refs_2_.1) | copy-start | bytes 1382404
  1.6 12.8 %copy-start.4 = (bf16[2,256,240]{2,1,0:T(8,128)(2,1)S(1)}, bf16[2,256,240]{2,1,0:T(8,128)(2,1)}, u32[]{:S(2)}) copy-start(bf16[2,256,240]{2,1,0:T(8,128)(2,1)} %constant.21.clone.refs_7_) | copy-start | bytes 737284
  1.6 12.8 %copy-start.5 = (bf16[2,256,240]{2,1,0:T(8,128)(2,1)S(1)}, bf16[2,256,240]{2,1,0:T(8,128)(2,1)}, u32[]{:S(2)}) copy-start(bf16[2,256,240]{2,1,0:T(8,128)(2,1)} %constant.20.clone.refs_6_) | copy-start | bytes 737284
  1.6 12.8 %copy-start.6 = (bf16[480,256]{1,0:T(8,128)(2,1)S(1)}, bf16[480,256]{1,0:T(8,128)(2,1)}, u32[]{:S(2)}) copy-start(bf16[480,256]{1,0:T(8,128)(2,1)} %constant.24.clone.refs_10_) | copy-start | bytes 737284
  1.6 12.8 %copy-start.7 = (bf16[2,240,256]{2,1,0:T(8,128)(2,1)S(1)}, bf16[2,240,256]{2,1,0:T(8,128)(2,1)}, u32[]{:S(2)}) copy-start(bf16[2,240,256]{2,1,0:T(8,128)(2,1)} %constant.19.clone.refs_5_) | copy-start | bytes 737284
  1.6 12.8 %copy-start.8 = (bf16[2,240,256]{2,1,0:T(8,128)(2,1)S(1)}, bf16[2,240,256]{2,1,0:T(8,128)(2,1)}, u32[]{:S(2)}) copy-start(bf16[2,240,256]{2,1,0:T(8,128)(2,1)} %constant.18.clone.refs_4_) | copy-start | bytes 737284
  1.6 12.8 %copy-start.10 = (bf16[128,480]{1,0:T(8,128)(2,1)S(1)}, bf16[128,480]{1,0:T(8,128)(2,1)}, u32[]{:S(2)}) copy-start(bf16[128,480]{1,0:T(8,128)(2,1)} %constant.22.clone.refs_8_) | copy-start | bytes 368644
  3.1 11.3 %copy-start.9 = (bf16[128,480]{1,0:T(8,128)(2,1)S(1)}, bf16[128,480]{1,0:T(8,128)(2,1)}, u32[]{:S(2)}) copy-start(bf16[128,480]{1,0:T(8,128)(2,1)} %constant.23.clone.refs_9_) | copy-start | bytes 368644
  3.1 9.6 %collective-permute-start = (bf16[256,128]{1,0:T(8,128)(2,1)S(1)}, bf16[256,128]{1,0:T(8,128)(2,1)S(1)}, u32[]{:S(2)}, u32[]{:S(2)}) collective-permute-start(bf16[256,128]{1,0:T(8,128)(2,1)S(1)} %spread.1.refs_0_), channel_id=1, source_target_pairs={{0,1},{1,0},{2,3},{3,2},{4,5},{5,4},{6,7},{7,6},{8,9},{9,8},{10,11... | collective-permute-start | bytes 196616 | tf_op jit(solution)/shard_map/ppermute | solution.py:319
  6.2 5.0 %collective-permute-start.2 = (bf16[2,1,80,128]{3,2,1,0:T(8,128)(2,1)S(1)}, bf16[2,1,80,128]{3,2,1,0:T(8,128)(2,1)S(1)}, u32[]{:S(2)}, u32[]{:S(2)}) collective-permute-start(bf16[2,1,80,128]{3,2,1,0:T(8,128)(2,1)S(1)} %copy-done), channel_id=1, source_target_pairs={{0,16},{2,18},{4,20},{6,22},{8,24},{10,26},{12,28},{14,30},{16,0},... | collective-permute-start | bytes 122888 | tf_op jit(solution)/shard_map/ppermute | solution.py:303
  8.7 4.0 %collective-permute-start.1 = (bf16[2,1,80,128]{3,2,1,0:T(8,128)(2,1)S(1)}, bf16[2,1,80,128]{3,2,1,0:T(8,128)(2,1)S(1)}, u32[]{:S(2)}, u32[]{:S(2)}) collective-permute-start(bf16[2,1,80,128]{3,2,1,0:T(8,128)(2,1)S(1)} %copy-done), channel_id=1, source_target_pairs={{0,24},{2,26},{4,28},{6,30},{8,0},{10,2},{12,4},{14,6},{16,8},{18,... | collective-permute-start | bytes 122888 | tf_op jit(solution)/shard_map/ppermute | solution.py:303
  12.8 4.9 %collective-permute-start.3 = (bf16[2,3,80,128]{3,2,1,0:T(8,128)(2,1)S(1)}, bf16[2,3,80,128]{3,2,1,0:T(8,128)(2,1)S(1)}, u32[]{:S(2)}, u32[]{:S(2)}) collective-permute-start(bf16[2,3,80,128]{3,2,1,0:T(8,128)(2,1)S(1)} %constant_dynamic-update-slice_fusion.refs_5_), channel_id=1, source_target_pairs={{0,4},{2,6},{4,0},{6,2},{8,12},{10,14},{12,8},{14,10},{16,20},{18,... | collective-permute-start | bytes 368648 | tf_op jit(solution)/shard_map/ppermute | solution.py:327
  17.7 5.0 %collective-permute-start.5 = (bf16[2,3,80,128]{3,2,1,0:T(8,128)(2,1)S(1)}, bf16[2,3,80,128]{3,2,1,0:T(8,128)(2,1)S(1)}, u32[]{:S(2)}, u32[]{:S(2)}) collective-permute-start(bf16[2,3,80,128]{3,2,1,0:T(8,128)(2,1)S(1)} %constant_dynamic-update-slice_fusion.refs_5_), channel_id=1, source_target_pairs={{0,2},{2,0},{4,6},{6,4},{8,10},{10,8},{12,14},{14,12},{16,18},{18,... | collective-permute-start | bytes 368648 | tf_op jit(solution)/shard_map/ppermute | solution.py:327
  17.7 5.0 %collective-permute-start.6 = (bf16[2,3,80,128]{3,2,1,0:T(8,128)(2,1)S(1)}, bf16[2,3,80,128]{3,2,1,0:T(8,128)(2,1)S(1)}, u32[]{:S(2)}, u32[]{:S(2)}) collective-permute-start(bf16[2,3,80,128]{3,2,1,0:T(8,128)(2,1)S(1)} %collective-permute-done.3.refs_7_), channel_id=1, source_target_pairs={{0,2},{2,0},{4,6},{6,4},{8,10},{10,8},{12,14},{14,12},{16,18},{18,... | collective-permute-start | bytes 368648 | tf_op jit(solution)/shard_map/ppermute | solution.py:327
  18.2 4.4 %collective-permute-start.4 = (f32[80,256]{1,0:T(8,128)S(1)}, f32[80,256]{1,0:T(8,128)S(1)}, u32[]{:S(2)}, u32[]{:S(2)}) collective-permute-start(f32[80,256]{1,0:T(8,128)S(1)} %bitcast.15), channel_id=1, source_target_pairs={{0,1},{1,0},{2,3},{3,2},{4,5},{5,4},{6,7},{7,6},{8,9},{9,8},{10,11... | collective-permute-start | bytes 245768 | tf_op jit(solution)/shard_map/ppermute | solution.py:356
where the time goes:
time: 36 us; the launch traced here: 35.8 us
  blocking collectives  11.4 us (32%)
  starting transfers between devices  9.6 us (27%)
  waiting for transfers between devices  8.07 us (22%)
  Pallas kernels  5 us (14%)
  local copies, waits for them, and re-layouts  0.94 us (3%)
  between operations  0.78 us (2%)
    all_to_all x1, blocking collectives, body(): lax.all_to_all(sums, ('ga', 'band'), split_axis=0, concat_axis=0, tiled=T...  11.4 us
    ppermute x2, starting transfers between devices, body(): near.append(lax.ppermute(orbitals, 'band', pairs))  3.94 us
    ppermute x1, waiting for transfers between devices, body(): partials.append(lax.ppermute(send[distance - 1], 'ga', pairs))  3.91 us
    ppermute x1, starting transfers between devices, body(): all_coeffs.append(lax.ppermute(coeffs, 'ga', pairs))  3.03 us
    ppermute x2, waiting for transfers between devices, body(): near.append(lax.ppermute(orbitals, 'band', pairs))  2.65 us
    ppermute x3, starting transfers between devices, widen(): lax.ppermute(part, 'band', pairs)  2.09 us
    pallas_call x1, Pallas kernels, body(): pl.pallas_call(run_grid, out_shape=(jax.ShapeDtypeStruct((slots, 2 * widt...  1.8 us
    ppermute x3, waiting for transfers between devices, widen(): lax.ppermute(part, 'band', pairs)  1.5 us
  transfers between devices with their start and end apart: 7, of which 4 were waited for; matrix products, arithmetic and copies ran while one was open for 0% of the time, Pallas kernels for 5%

commit v1 on v0

v1 whole, which is shorter than its diff:
```python
import functools
import math

import jax
import jax.numpy as jnp
import numpy as np
from jax import lax
from jax.experimental import pallas as pl
from jax.experimental.pallas import tpu as pltpu
from jax.sharding import PartitionSpec as P


F32 = jnp.float32
BF16 = jnp.bfloat16
VMEM_SPEC = pl.BlockSpec(memory_space=pltpu.VMEM)
SMEM_SPEC = pl.BlockSpec(memory_space=pltpu.SMEM)
FIRST_FLOPS = 3_000_000_000
SPREAD_FLOPS = 1_500_000_000
GRID_FLOPS = 3_000_000_000
KERNEL_PARAMS = pltpu.CompilerParams(vmem_limit_bytes=16 * 1024 * 1024)


def hi_lo_table(values):
    high = jnp.asarray(values, F32).astype(BF16)
    high_np = np.asarray(values, np.float32).astype(jnp.bfloat16)
    low_np = (values - high_np.astype(np.float64)).astype(jnp.bfloat16)
    return high_np, low_np


def twiddle_tables(points, radius, group_count):
    width = 2 * radius
    planes = points // group_count
    z = np.arange(points, dtype=np.int64)
    gz = np.arange(width, dtype=np.int64) - radius + 1
    angle_z = (z[:, None] * gz[None, :] % points) * (2.0 * np.pi / points)
    forward = np.concatenate([np.cos(angle_z), np.sin(angle_z)], axis=1)
    forward = forward.reshape(group_count, planes, 2 * width)
    backward = np.ascontiguousarray(np.transpose(forward, (0, 2, 1)))
    gx = np.arange(radius, dtype=np.int64)
    angle_x = (gx[:, None] * z[None, :] % points) * (2.0 * np.pi / points)
    x_table = np.concatenate([np.cos(angle_x), np.sin(angle_x)], axis=0)
    z_high, z_low = hi_lo_table(forward)
    zt_high, zt_low = hi_lo_table(backward)
    x_high, x_low = hi_lo_table(x_table)
    xt = np.concatenate([x_high.T, x_low.T], axis=1)
    return np.stack([z_high, z_low], 1), np.stack([zt_high, zt_low], 1), np.stack([x_high, x_low]), xt


def split(values):
    high = values.astype(BF16)
    low = (values - high.astype(F32)).astype(BF16)
    return high, low


def dot(left, right):
    return jnp.dot(left, right, preferred_element_type=F32)


def dot_rows(left, right):
    return lax.dot_general(left, right, (((1,), (1,)), ((), ())), preferred_element_type=F32)


class Bands:
    def __init__(self, total):
        self.total = total
        self.inner = math.gcd(total, 4)
        self.blocks = total // self.inner
        self.ny = max(self.inner // 2, 1)
        self.nc = min(self.inner, 2)
        self.parts = [(s, y) for y in range(self.ny) for s in range((self.blocks + 1) // 2)]
        self.half = self.blocks // 2 if self.blocks % 2 == 0 else 0
        if self.half:
            self.parts.append(None)
        self.count = len(self.parts) * self.nc

    def source(self, device, part, other_core, where=np.where):
        block = device // self.inner if where is np.where else lax.div(device, self.inner)
        place = device - block * self.inner
        if self.parts[part] is None:
            turned = where(block < self.half, self.ny - 1, 0)
            block = where(block < self.half, block + self.half, block - self.half)
        else:
            shift, turned = self.parts[part]
            block = where(block < shift, block - shift + self.blocks, block - shift)
        return block * self.inner + (place ^ (turned * self.nc + other_core))

    def pairs(self, part):
        return [(int(self.source(device, part, 0)), device) for device in range(self.total)]


def canonical_lane(sticks, radius):
    gx = sticks - radius + 1
    return jnp.where(gx >= 0, gx, radius - gx)


def rows_kernel(out_ref):
    out_ref[...] = lax.broadcasted_iota(jnp.int32, out_ref.shape, 0).astype(F32)


def copy_kernel(_, in_ref, out_ref):
    out_ref[...] = in_ref[...]


def sticks_of(sticks_ref, group, slots):
    sticks = sticks_ref[...]
    row = sticks[:, :slots]
    for index in range(1, sticks.shape[1] // slots):
        row = jnp.where(group == index, sticks[:, index * slots : (index + 1) * slots], row)
    return row


def spread(values, inverse):
    index = jnp.maximum(inverse, 0)
    parts = []
    for part in values:
        moved = jnp.take_along_axis(part.astype(F32), index, axis=1, mode="promise_in_bounds")
        parts.append(jnp.where(inverse >= 0, moved, 0.0))
    return jnp.concatenate(parts, axis=1).astype(BF16)


def choose_slots(sticks_ref, group, slots, width):
    lane = canonical_lane(sticks_of(sticks_ref, group, slots), width // 2)
    return (lax.broadcasted_iota(jnp.int32, (width, slots), 0) == lane).astype(F32).astype(BF16)


def group_before(ga, distance, groups):
    return lax.rem(ga + (groups - distance), groups)


def place_kernel(ga_ref, rows_ref, orbitals_ref, entries_ref, out_ref, inverse_ref, e_ref, all_ref):
    width = entries_ref.shape[1]
    slots = orbitals_ref.shape[2]
    total = entries_ref.shape[0]
    groups = total // slots
    ga = ga_ref[0]
    chunks, _, lanes = e_ref.shape
    lists_t = entries_ref[...].astype(F32)
    if chunks * lanes > total:
        lists_t = jnp.concatenate([lists_t, jnp.full((chunks * lanes - total, width), -1.0, F32)], axis=0)
    position = rows_ref[...]
    for chunk in range(chunks):
        e_ref[chunk] = lists_t[chunk * lanes : (chunk + 1) * lanes].T

        def step(k, found):
            match = e_ref[chunk, pl.ds(k, 1), :] == position
            return jnp.where(match, k.astype(F32), found)

        found = lax.fori_loop(0, width, step, jnp.full((width, lanes), -1.0, F32), unroll=8)
        all_ref[chunk * lanes : (chunk + 1) * lanes, :] = found.T.astype(jnp.int32)

    def lists(group):
        return all_ref[pl.ds(pl.multiple_of(group * slots, 8), slots), :]

    out_ref[...] = spread([orbitals_ref[0, 0], orbitals_ref[1, 0]], lists(ga))
    for distance in range(1, groups):
        inverse_ref[distance - 1] = lists(group_before(ga, distance, groups))


def grid_kernel(ga_ref, other_refs, own_coeffs_ref, inverse_ref, potential_ref, sticks_ref, tables, own_ref, send_ref):
    z_table, zt_table, x_table, xt = tables
    planes, _ = potential_ref.shape
    width = own_coeffs_ref.shape[1] // 2
    radius = width // 2
    slots = own_ref.shape[0]
    groups = sticks_ref.shape[1] // slots
    ga = ga_ref[0]
    coeffs = dot(choose_slots(sticks_ref, ga, slots, width), own_coeffs_ref[...])
    for distance, ref in enumerate(other_refs, 1):
        choose = choose_slots(sticks_ref, group_before(ga, distance, groups), slots, width)
        coeffs = coeffs + dot(choose, spread([ref[0, 0], ref[1, 0]], inverse_ref[distance - 1]))
    real_part, imag_part = coeffs[:, :width], coeffs[:, width:]
    rows = jnp.concatenate(
        [
            jnp.concatenate([real_part, -imag_part], axis=1),
            jnp.concatenate([imag_part, real_part], axis=1),
        ],
        axis=0,
    ).astype(BF16)
    columns = dot_rows(z_table[ga, 0], rows) + dot_rows(z_table[ga, 1], rows)
    col_re, col_im = columns[:, :width], columns[:, width:]
    rol_re, rol_im = pltpu.roll(col_re, radius, 1), pltpu.roll(col_im, radius, 1)
    even = lax.broadcasted_iota(jnp.int32, (planes, width), 1) < radius
    parity = jnp.concatenate(
        [
            jnp.where(even, col_re + rol_re, col_im - rol_im),
            jnp.where(even, col_im + rol_im, rol_re - col_re),
        ],
        axis=0,
    )
    par_high, par_low = split(parity)
    table = x_table[0]
    field = dot(jnp.concatenate([par_high, par_low], axis=1), jnp.concatenate([table, table], axis=0))
    field = field + dot(par_high, x_table[1])
    values = potential_ref[...]
    product = jnp.concatenate([values, values], axis=0) * field
    prod_high, prod_low = split(product)
    table_t = xt[...]
    wide = dot(prod_high, table_t)
    back = wide[:, :width] + wide[:, width:] + dot(prod_low, table_t[:, :width])
    back_re, back_im = back[:planes], back[planes:]
    rol_re, rol_im = pltpu.roll(back_re, radius, 1), pltpu.roll(back_im, radius, 1)
    gathered = jnp.concatenate(
        [
            jnp.where(even, back_re + rol_im, rol_re - back_im),
            jnp.where(even, back_im - rol_re, rol_im + back_re),
        ],
        axis=1,
    )
    gat_high, gat_low = split(gathered)
    spectra = dot(zt_table[ga, 0], gat_high) + dot(zt_table[ga, 1], gat_high) + dot(zt_table[ga, 0], gat_low)
    spectra = jnp.concatenate(
        [
            spectra[:width, :width] + spectra[width:, width:],
            spectra[:width, width:] - spectra[width:, :width],
        ],
        axis=0,
    )
    spec_high, spec_low = split(spectra)
    spec = jnp.concatenate([spec_high, spec_low], axis=1)
    lanes = lax.broadcasted_iota(jnp.int32, (slots, width), 1)
    for distance in range(groups):
        group = lax.rem(ga + distance, groups)
        lane_row = canonical_lane(sticks_of(sticks_ref, group, slots), radius).astype(F32)
        lane_col = jnp.broadcast_to(lane_row, (width, slots)).T.astype(jnp.int32)
        choose = (lane_col == lanes).astype(F32).astype(BF16)
        picked = dot_rows(jnp.concatenate([choose, choose], axis=1), spec)
        if distance == 0:
            own_ref[...] = picked
        else:
            send_ref[distance - 1] = picked


def apply_part(ga, partial_refs, orbitals_ref, entries_ref, sticks_ref, points):
    width = entries_ref.shape[1]
    slots = orbitals_ref.shape[2]
    radius = width // 2
    total = partial_refs[0][...]
    for ref in partial_refs[1:]:
        total = total + ref[...]
    entries = entries_ref[pl.ds(pl.multiple_of(ga * slots, 8), slots), :]
    present = entries >= 0
    index = jnp.maximum(entries, 0)
    gx_row = (sticks_of(sticks_ref, ga, entries.shape[0]) - radius + 1).astype(F32)
    gx = jnp.broadcast_to(gx_row, (width, gx_row.shape[1])).T
    gz = (entries - radius + 1).astype(F32)
    kinetic = (gx * gx + gz * gz) * (1.0 / (radius * radius))
    result = []
    for part in range(2):
        picked = jnp.take_along_axis(
            total[:, part * width : (part + 1) * width], index, axis=1, mode="promise_in_bounds"
        )
        value = kinetic * orbitals_ref[part, 0].astype(F32) + picked * (1.0 / (points * points))
        result.append(jnp.where(present, value, 0.0).astype(BF16))
    return result, present


def final_kernel(points, ga_ref, partial_refs, orbitals_ref, entries_ref, sticks_ref, psi_refs, out_ref, sums_ref):
    ga = ga_ref[0]
    result, present = apply_part(ga, partial_refs, orbitals_ref, entries_ref, sticks_ref, points)
    for part in range(2):
        out_ref[part, 0] = result[part]
    _, width = present.shape
    h_re, h_im = result[0].astype(F32), result[1].astype(F32)
    m_re = jnp.where(present, orbitals_ref[0, 0].astype(F32), 0.0)
    m_im = jnp.where(present, orbitals_ref[1, 0].astype(F32), 0.0)
    rows = [[], [], [], []]
    for part in range(psi_refs[0].shape[1]):
        for psi_ref in psi_refs:
            left_re = psi_ref[0, part].astype(F32)
            left_im = psi_ref[1, part].astype(F32)
            for place, (right_re, right_im) in enumerate(((m_re, m_im), (h_re, h_im))):
                rows[2 * place].append(jnp.sum(left_re * right_re + left_im * right_im, axis=0, keepdims=True))
                rows[2 * place + 1].append(jnp.sum(left_re * right_im - left_im * right_re, axis=0, keepdims=True))
    flat = sum(rows, [])
    lanes = sums_ref.shape[1]
    if len(flat) < lanes:
        flat.append(jnp.zeros((lanes - len(flat), width), F32))
    sums = jnp.sum(jnp.concatenate(flat, axis=0).T, axis=0, keepdims=True)
    sums_ref[...] = jnp.broadcast_to(sums, sums_ref.shape)


def assemble_kernel(groups, layout, scale, sums_ref, corr_ref, ham_ref):
    bands = layout.total
    total = sums_ref[0:bands, :]
    for group in range(1, groups):
        total = total + sums_ref[group * bands : (group + 1) * bands, :]
    lanes = total.shape[1]
    total = jnp.concatenate([total, jnp.zeros((lanes - bands, lanes), F32)], axis=0).T * scale
    row = lax.broadcasted_iota(jnp.int32, (bands, lanes), 0)
    col = lax.broadcasted_iota(jnp.int32, (bands, lanes), 1)
    matches = []
    for part in range(len(layout.parts)):
        for core in range(layout.nc):
            matches.append(row == layout.source(col, part, core, jnp.where))
    covered = functools.reduce(jnp.logical_or, matches)
    for place, ref in enumerate((corr_ref, ham_ref)):
        for part in range(2):
            base = (2 * place + part) * layout.count
            direct = jnp.zeros((bands, lanes), F32)
            for index, match in enumerate(matches):
                direct = jnp.where(match, total[base + index : base + index + 1, :], direct)
            padded = jnp.concatenate([direct, jnp.zeros((lanes - bands, lanes), F32)], axis=0)
            mirror = padded.T[:bands]
            if part:
                mirror = -mirror
            ref[part] = jnp.where(covered, direct, mirror)[:, :bands]


def general_matrices(psi, masked, applied, layout, scale):
    bands, count = layout.total, layout.count
    left = psi.reshape(2, count, -1)
    right = jnp.stack([masked.reshape(2, -1), applied.reshape(2, -1)])
    product = jnp.einsum("cin,mdn->mcdi", left, right, preferred_element_type=F32)
    block = jnp.stack([product[:, 0, 0] + product[:, 1, 1], product[:, 0, 1] - product[:, 1, 0]], axis=1)
    everywhere = lax.all_gather(lax.psum(block * scale, "ga"), "band", axis=0)
    slot = np.full((bands, bands), -1)
    for device in range(bands):
        for part in range(len(layout.parts)):
            for core in range(layout.nc):
                slot[device, layout.source(device, part, core)] = part * layout.nc + core
    flat = jnp.transpose(everywhere, (1, 2, 0, 3)).reshape(4 * bands, count)
    index = jnp.asarray(np.tile(np.maximum(slot, 0), (4, 1)), jnp.int32)
    direct = jnp.take_along_axis(flat, index, axis=1).reshape(2, 2, bands, bands)
    direct = jnp.swapaxes(direct, 2, 3)
    sign = jnp.asarray([1.0, -1.0], F32)[None, :, None, None]
    full = jnp.where(jnp.asarray(slot.T >= 0), direct, sign * jnp.swapaxes(direct, 2, 3))
    return full[0], full[1]


def body(band_total, groups, orbitals, potential, slot_sticks, stick_entries):
    _, points = potential.shape
    width = stick_entries.shape[1]
    radius = width // 2
    slots = orbitals.shape[2]
    layout = Bands(band_total)
    ga = lax.axis_index("ga").astype(jnp.int32).reshape(1)
    sticks = slot_sticks.reshape(1, groups * slots)
    tables = [jnp.asarray(t) for t in twiddle_tables(points, radius, groups)]

    rows = pl.pallas_call(
        rows_kernel,
        out_shape=jax.ShapeDtypeStruct((width, 128), F32),
        out_specs=VMEM_SPEC,
        compiler_params=KERNEL_PARAMS,
        cost_estimate=pl.CostEstimate(flops=FIRST_FLOPS, bytes_accessed=0, transcendentals=0),
        name="rows",
    )()
    sticks = pl.pallas_call(
        copy_kernel,
        out_shape=jax.ShapeDtypeStruct(sticks.shape, jnp.int32),
        in_specs=[VMEM_SPEC, VMEM_SPEC],
        out_specs=VMEM_SPEC,
        compiler_params=KERNEL_PARAMS,
        name="sticks",
    )(rows, sticks)
    orbitals, rows, sticks = lax.optimization_barrier((orbitals, rows, sticks))
    others = []
    for distance in range(1, groups):
        pairs = [(i, (i + distance) % groups) for i in range(groups)]
        others.append(lax.ppermute(orbitals, "ga", pairs))
    near, far = [orbitals], []
    for part, way in enumerate(layout.parts):
        if way is None or (way[1] == 0 and part > 0):
            (far if way is None else near).append(lax.ppermute(orbitals, "band", layout.pairs(part)))

    chunks = pl.cdiv(groups * slots, 128)
    place = pl.pallas_call(
        place_kernel,
        out_shape=(
            jax.ShapeDtypeStruct((slots, 2 * width), BF16),
            jax.ShapeDtypeStruct((groups - 1, slots, width), jnp.int32),
        ),
        in_specs=[SMEM_SPEC] + [VMEM_SPEC] * 3,
        out_specs=(VMEM_SPEC, VMEM_SPEC),
        scratch_shapes=[pltpu.VMEM((chunks, width, 128), F32), pltpu.VMEM((chunks * 128, width), jnp.int32)],
        compiler_params=KERNEL_PARAMS,
        cost_estimate=pl.CostEstimate(flops=SPREAD_FLOPS, bytes_accessed=0, transcendentals=0),
        name="place",
    )
    coeffs, inverse = place(ga, rows, orbitals, stick_entries)
    coeffs, *arrived = lax.optimization_barrier((coeffs, *near, *far))
    near, far = jnp.concatenate(arrived[: len(near)], axis=1), arrived[len(near) :]
    psi = [near]
    if layout.ny == 2:
        pairs = [(i, i ^ layout.nc) for i in range(band_total)]
        psi.append(lax.ppermute(near, "band", pairs))

    def run_grid(ga_ref, *refs):
        count = len(others)
        grid_kernel(ga_ref, refs[:count], *refs[count : count + 4], refs[count + 4 : count + 8], *refs[count + 8 :])

    grid = pl.pallas_call(
        run_grid,
        out_shape=(
            jax.ShapeDtypeStruct((slots, 2 * width), F32),
            jax.ShapeDtypeStruct((groups - 1, slots, 2 * width), F32),
        ),
        in_specs=[SMEM_SPEC] + [VMEM_SPEC] * (len(others) + 8),
        out_specs=(VMEM_SPEC, VMEM_SPEC),
        compiler_params=KERNEL_PARAMS,
        cost_estimate=pl.CostEstimate(flops=GRID_FLOPS, bytes_accessed=0, transcendentals=0),
        name="grid",
    )
    own, send = grid(ga, *others, coeffs, inverse, potential, sticks, *tables)
    psi = [jnp.concatenate(psi + far, axis=1)]
    if layout.nc == 2:
        psi.append(lax.ppermute(psi[0], "band", [(i, i ^ 1) for i in range(band_total)]))
    partials = [own]
    for distance in range(1, groups):
        pairs = [(i, (i + distance) % groups) for i in range(groups)]
        partials.append(lax.ppermute(send[distance - 1], "ga", pairs))

    scale = 1.0 / (4.0 * radius * radius)
    out_type = jax.ShapeDtypeStruct(orbitals.shape, BF16)
    small = 4 * layout.count <= 128 and band_total <= 128
    count = len(partials)
    if not small:

        def run_apply(ga_ref, *refs):
            result, _ = apply_part(ga_ref[0], refs[:count], *refs[count : count + 3], points)
            refs[count + 3][0, 0] = result[0]
            refs[count + 3][1, 0] = result[1]

        applied = pl.pallas_call(
            run_apply,
            out_shape=out_type,
            in_specs=[SMEM_SPEC] + [VMEM_SPEC] * (count + 3),
            out_specs=VMEM_SPEC,
            compiler_params=KERNEL_PARAMS,
            name="apply",
        )(ga, *partials, orbitals, stick_entries, sticks)
        own_lists = lax.dynamic_slice_in_dim(stick_entries, ga[0] * slots, slots, 0)
        masked = jnp.where(own_lists >= 0, orbitals, jnp.zeros_like(orbitals))
        correlation, reduced = general_matrices(jnp.stack(psi, axis=2), masked, applied, layout, scale)
        return applied, correlation, reduced

    def run_final(ga_ref, *refs):
        psi_refs, outs = refs[count + 3 : count + 3 + len(psi)], refs[count + 3 + len(psi) :]
        final_kernel(points, ga_ref, refs[:count], *refs[count : count + 3], psi_refs, *outs)

    applied, sums = pl.pallas_call(
        run_final,
        out_shape=(out_type, jax.ShapeDtypeStruct((groups * band_total, 128), F32)),
        in_specs=[SMEM_SPEC] + [VMEM_SPEC] * (count + 3 + len(psi)),
        out_specs=(VMEM_SPEC, VMEM_SPEC),
        compiler_params=KERNEL_PARAMS,
        name="final",
    )(ga, *partials, orbitals, stick_entries, sticks, *psi)
    everywhere = lax.all_to_all(sums, ("ga", "band"), split_axis=0, concat_axis=0, tiled=True)
    matrix = jax.ShapeDtypeStruct((2, band_total, band_total), F32)

    def run_assemble(sums_ref, corr_ref, ham_ref):
        assemble_kernel(groups, layout, scale, sums_ref, corr_ref, ham_ref)

    correlation, reduced = pl.pallas_call(
        run_assemble,
        out_shape=(matrix, matrix),
        in_specs=[VMEM_SPEC],
        out_specs=(VMEM_SPEC, VMEM_SPEC),
        compiler_params=KERNEL_PARAMS,
        name="assemble",
    )(everywhere)
    return applied, correlation, reduced


def solution(mesh):
    band_total = mesh.shape["band"]
    groups = mesh.shape["ga"]

    def mapped(orbitals, potential, slot_sticks, stick_entries):
        return body(band_total, groups, orbitals, potential, slot_sticks, stick_entries)

    return jax.shard_map(
        mapped,
        mesh=mesh,
        in_specs=(P(None, "band", "ga", None), P("ga", None), P(), P()),
        out_specs=(P(None, "band", "ga", None), P(), P()),
        check_vma=False,
    )
```

time: 36 us -> 34.6 us (0.961)
  waiting for transfers between devices: 8.07 us -> 6.73 us
  blocking collectives: 11.4 us -> 10.7 us
  starting transfers between devices: 9.6 us -> 10.1 us
    ppermute x1, starting transfers between devices: 0.53 us -> 1.56 us  [body(): partials.append(lax.ppermute(send[distance - 1], 'ga', pairs))]
    all_to_all x1, blocking collectives: 11.4 us -> 10.7 us  [body(): lax.all_to_all(sums, ('ga', 'band'), split_axis=0, concat_axis=0, tiled=T...]
    ppermute x6 -> x5, waiting for transfers between devices: 4.16 us -> 3.4 us  [the longest x1 3.13 us: body(): psi.append(lax.ppermute(near, 'band', pairs))]
    ppermute x1, waiting for transfers between devices: 3.91 us -> 3.33 us  [body(): partials.append(lax.ppermute(send[distance - 1], 'ga', pairs))]
    ppermute x6 -> x5, starting transfers between devices: 9.06 us -> 8.57 us  [the longest x2 5.64 us: body(): lax.ppermute(orbitals, 'band', layout.pairs(part))]
    pallas_call x3 -> x4, Pallas kernels: 3.31 us -> 3.59 us  [the longest x1 1.91 us: body(): own, send = grid(ga, *others, coeffs, inverse, potential, sticks, *tables)]
    unnamed x24 -> x19, local copies, waits for them, and re-layouts: 0.93 us -> 0.85 us
  transfers between devices with their start and end apart: 7 -> 6, of which waited for: 4 -> 3; matrix products, arithmetic and copies ran while one was open for 0% -> 0% of each run, Pallas kernels for 5% -> 10%
where the time goes in v1:
time: 34.6 us; the launch traced here: 34.4 us
  blocking collectives  10.7 us (31%)
  starting transfers between devices  10.1 us (29%)
  waiting for transfers between devices  6.73 us (19%)
  Pallas kernels  5.27 us (15%)
  local copies, waits for them, and re-layouts  0.86 us (2%)
  between operations  0.78 us (2%)
    all_to_all x1, blocking collectives, body(): lax.all_to_all(sums, ('ga', 'band'), split_axis=0, concat_axis=0, tiled=T...  10.7 us
    ppermute x2, starting transfers between devices, body(): lax.ppermute(orbitals, 'band', layout.pairs(part))  5.64 us
    ppermute x1, waiting for transfers between devices, body(): partials.append(lax.ppermute(send[distance - 1], 'ga', pairs))  3.33 us
    ppermute x1, waiting for transfers between devices, body(): psi.append(lax.ppermute(near, 'band', pairs))  3.13 us
    pallas_call x1, Pallas kernels, body(): own, send = grid(ga, *others, coeffs, inverse, potential, sticks, *tables)  1.91 us
    pallas_call x1, Pallas kernels, body(): coeffs, inverse = place(ga, rows, orbitals, stick_entries)  1.66 us
    ppermute x1, starting transfers between devices, body(): partials.append(lax.ppermute(send[distance - 1], 'ga', pairs))  1.56 us
    ppermute x1, starting transfers between devices, body(): others.append(lax.ppermute(orbitals, 'ga', pairs))  1.49 us
  transfers between devices with their start and end apart: 6, of which 3 were waited for; matrix products, arithmetic and copies ran while one was open for 0% of the time, Pallas kernels for 10%

profile of v1, /device:TPU:0, one launch (start us, length us, event | category | flops | bytes accessed | tf_op | source)
XLA Modules:
  0.0 34.4 jit_solution(7714866851351083203)
XLA Ops:
  0.6 0.0 copy-start.1
  0.6 0.0 copy-start.2
  0.7 0.0 copy-start
  0.7 0.7 %copy-done.2 = s32[160]{0:T(256)S(1)} copy-done((s32[160]{0:T(256)S(1)}, s32[160]{0:T(256)}, u32[]{:S(2)}) %copy-start.2) | copy-done | bytes 664
  1.4 0.1 copy-done
  1.5 3.1 %collective-permute-start.1 = (bf16[2,1,80,128]{3,2,1,0:T(8,128)(2,1)S(1)}, bf16[2,1,80,128]{3,2,1,0:T(8,128)(2,1)S(1)}, u32[]{:S(2)}, u32[]{:S(2)}) collective-permute-start(bf16[2,1,80,128]{3,2,1,0:T(8,128)(2,1)S(1)} %copy-done), channel_id=1, source_target_pairs={{24,0},{26,2},{28,4},{30,6},{0,8},{2,10},{4,12},{6,14},{8,16},{10,... | collective-permute-start | bytes 122888 | tf_op jit(solution)/shard_map/ppermute | solution.py:364
  4.5 2.6 %collective-permute-start.2 = (bf16[2,1,80,128]{3,2,1,0:T(8,128)(2,1)S(1)}, bf16[2,1,80,128]{3,2,1,0:T(8,128)(2,1)S(1)}, u32[]{:S(2)}, u32[]{:S(2)}) collective-permute-start(bf16[2,1,80,128]{3,2,1,0:T(8,128)(2,1)S(1)} %copy-done), channel_id=1, source_target_pairs={{20,0},{22,2},{16,4},{18,6},{28,8},{30,10},{24,12},{26,14},{0,16},... | collective-permute-start | bytes 122888 | tf_op jit(solution)/shard_map/ppermute | solution.py:364
  7.1 1.5 %collective-permute-start = (bf16[2,1,80,128]{3,2,1,0:T(8,128)(2,1)S(1)}, bf16[2,1,80,128]{3,2,1,0:T(8,128)(2,1)S(1)}, u32[]{:S(2)}, u32[]{:S(2)}) collective-permute-start(bf16[2,1,80,128]{3,2,1,0:T(8,128)(2,1)S(1)} %copy-done), channel_id=1, source_target_pairs={{0,1},{1,0},{2,3},{3,2},{4,5},{5,4},{6,7},{7,6},{8,9},{9,8},{10,11... | collective-permute-start | bytes 122888 | tf_op jit(solution)/shard_map/ppermute | solution.py:360
  8.6 0.0 copy-start.7
  8.6 1.7 %place.1 = (bf16[80,256]{1,0:T(8,128)(2,1)S(1)}, s32[1,80,128]{2,1,0:T(8,128)S(1)}) custom-call(s32[1]{0:T(128)} %bitcast.ga_ref, f32[128,128]{1,0:T(8,128)S(1)} %rows.1._.rows_ref, bf16[2,1,80,128]{3,2,1,0:T(8,128)(2,1)S(1)} %copy-done, s32[160,128]{1,0:T(8,128)S(1)} %copy-done.1), custom_call_target="tpu_custom_call" | custom-call | flops 1500000000 | tf_op jit(solution)/shard_map/place/pallas_call | solution.py:380
  10.3 0.0 copy-start.3
  10.3 0.0 collective-permute-done.1
  10.3 0.3 collective-permute-done.2
  10.6 1.4 %collective-permute-start.4 = (bf16[2,2,80,128]{3,2,1,0:T(8,128)(2,1)S(1)}, bf16[2,2,80,128]{3,2,1,0:T(8,128)(2,1)S(1)}, u32[]{:S(2)}, u32[]{:S(2)}) collective-permute-start(bf16[2,2,80,128]{3,2,1,0:T(8,128)(2,1)S(1)} %pad_maximum_fusion), channel_id=1, source_target_pairs={{0,4},{2,6},{4,0},{6,2},{8,12},{10,14},{12,8},{14,10},{16,20},{18,... | collective-permute-start | bytes 245768 | tf_op jit(solution)/shard_map/ppermute | solution.py:386
  12.0 3.1 %collective-permute-done.4 = bf16[2,2,80,128]{3,2,1,0:T(8,128)(2,1)S(1)} collective-permute-done((bf16[2,2,80,128]{3,2,1,0:T(8,128)(2,1)S(1)}, bf16[2,2,80,128]{3,2,1,0:T(8,128)(2,1)S(1)}, u32[]{:S(2)}, u32[]{:S(2)}) %collective-permute-start.4) | collective-permute-done | bytes 81952 | tf_op jit(solution)/shard_map/ppermute | solution.py:386
  15.1 0.1 collective-permute-start.5
  15.2 0.0 collective-permute-done.refs_0_
  15.3 1.9 %grid.1 = (f32[80,256]{1,0:T(8,128)S(1)}, f32[1,80,256]{2,1,0:T(8,128)S(1)}) custom-call(s32[1]{0:T(128)} %bitcast.ga_ref, bf16[2,1,80,128]{3,2,1,0:T(8,128)(2,1)S(1)} %collective-permute-done.refs_0_, bf16[80,256]{1,0:T(8,128)(2,1)S(1)} %get-tuple-element.21.refs_1_, s32[1,80,128]{2,1,0:T(8,128)S(1)} %get-tuple-element.22.refs_2_, ...), custom_call_target="tpu_custom_call" | custom-call | flops 3000000000 | tf_op jit(solution)/shard_map/grid/pallas_call | solution.py:404
  17.2 1.6 %collective-permute-start.3 = (f32[80,256]{1,0:T(8,128)S(1)}, f32[80,256]{1,0:T(8,128)S(1)}, u32[]{:S(2)}, u32[]{:S(2)}) collective-permute-start(f32[80,256]{1,0:T(8,128)S(1)} %bitcast.10), channel_id=1, source_target_pairs={{0,1},{1,0},{2,3},{3,2},{4,5},{5,4},{6,7},{7,6},{8,9},{9,8},{10,11... | collective-permute-start | bytes 245768 | tf_op jit(solution)/shard_map/ppermute | solution.py:411
  18.7 3.3 %collective-permute-done.3.refs_1_ = f32[80,256]{1,0:T(8,128)S(1)} collective-permute-done((f32[80,256]{1,0:T(8,128)S(1)}, f32[80,256]{1,0:T(8,128)S(1)}, u32[]{:S(2)}, u32[]{:S(2)}) %collective-permute-start.3) | collective-permute-done | bytes 81952 | tf_op jit(solution)/shard_map/ppermute | solution.py:411
  22.1 0.0 collective-permute-done.5.refs_6_
  22.1 0.9 %final.1 = (bf16[2,1,80,128]{3,2,1,0:T(8,128)(2,1)}, f32[32,128]{1,0:T(8,128)S(1)}) custom-call(s32[1]{0:T(128)} %bitcast.ga_ref, f32[80,256]{1,0:T(8,128)S(1)} %get-tuple-element.24.refs_0_, f32[80,256]{1,0:T(8,128)S(1)} %collective-permute-done.3.refs_1_, bf16[2,1,80,128]{3,2,1,0:T(8,128)(2,1)S(1)} %copy-done, s32[160,128]{1,0:T(8,128)S(1)} %copy-done.1, ...), custom_call_target="tpu_custom_call" | custom-call | tf_op jit(solution)/shard_map/final/pallas_call | solution.py:441
  23.0 10.7 %all_to_all.11 = f32[32,1,128]{2,1,0:T(1,128)S(1)} all-to-all(f32[32,1,128]{2,1,0:T(1,128)S(1)} %bitcast.8), channel_id=1, replica_groups=mesh['band'=16,'ga'=2] {'ga','band'}, dimensions={0} | all-to-all | bytes 32768 | tf_op jit(solution)/shard_map/all_to_all | solution.py:449
  33.7 0.8 %assemble.1 = (f32[2,16,16]{2,1,0:T(8,128)}, f32[2,16,16]{2,1,0:T(8,128)}) custom-call(f32[32,128]{1,0:T(8,128)S(1)} %bitcast.7), custom_call_target="tpu_custom_call" | custom-call | tf_op jit(solution)/shard_map/assemble/pallas_call | solution.py:455
  (16 shorter events, 0.1 us)
Async XLA Ops:
  0.6 8.0 %copy-start.1 = (s32[160,128]{1,0:T(8,128)S(1)}, s32[160,128]{1,0:T(8,128)}, u32[]{:S(2)}) copy-start(s32[160,128]{1,0:T(8,128)} %refs_3_.3) | copy-start | bytes 245764
  0.6 0.7 %copy-start.2 = (s32[160]{0:T(256)S(1)}, s32[160]{0:T(256)}, u32[]{:S(2)}) copy-start(s32[160]{0:T(256)} %param.10) | copy-start | bytes 1924
  0.7 0.8 %copy-start = (bf16[2,1,80,128]{3,2,1,0:T(8,128)(2,1)S(1)}, bf16[2,1,80,128]{3,2,1,0:T(8,128)(2,1)}, u32[]{:S(2)}) copy-start(bf16[2,1,80,128]{3,2,1,0:T(8,128)(2,1)} %refs_2_) | copy-start | bytes 122884
  1.5 8.8 %collective-permute-start.1 = (bf16[2,1,80,128]{3,2,1,0:T(8,128)(2,1)S(1)}, bf16[2,1,80,128]{3,2,1,0:T(8,128)(2,1)S(1)}, u32[]{:S(2)}, u32[]{:S(2)}) collective-permute-start(bf16[2,1,80,128]{3,2,1,0:T(8,128)(2,1)S(1)} %copy-done), channel_id=1, source_target_pairs={{24,0},{26,2},{28,4},{30,6},{0,8},{2,10},{4,12},{6,14},{8,16},{10,... | collective-permute-start | bytes 122888 | tf_op jit(solution)/shard_map/ppermute | solution.py:364
  4.5 6.1 %collective-permute-start.2 = (bf16[2,1,80,128]{3,2,1,0:T(8,128)(2,1)S(1)}, bf16[2,1,80,128]{3,2,1,0:T(8,128)(2,1)S(1)}, u32[]{:S(2)}, u32[]{:S(2)}) collective-permute-start(bf16[2,1,80,128]{3,2,1,0:T(8,128)(2,1)S(1)} %copy-done), channel_id=1, source_target_pairs={{20,0},{22,2},{16,4},{18,6},{28,8},{30,10},{24,12},{26,14},{0,16},... | collective-permute-start | bytes 122888 | tf_op jit(solution)/shard_map/ppermute | solution.py:364
  7.1 8.1 %collective-permute-start = (bf16[2,1,80,128]{3,2,1,0:T(8,128)(2,1)S(1)}, bf16[2,1,80,128]{3,2,1,0:T(8,128)(2,1)S(1)}, u32[]{:S(2)}, u32[]{:S(2)}) collective-permute-start(bf16[2,1,80,128]{3,2,1,0:T(8,128)(2,1)S(1)} %copy-done), channel_id=1, source_target_pairs={{0,1},{1,0},{2,3},{3,2},{4,5},{5,4},{6,7},{7,6},{8,9},{9,8},{10,11... | collective-permute-start | bytes 122888 | tf_op jit(solution)/shard_map/ppermute | solution.py:360
  8.6 6.6 %copy-start.4 = (bf16[2,2,256,240]{3,2,1,0:T(8,128)(2,1)S(1)}, bf16[2,2,256,240]{3,2,1,0:T(8,128)(2,1)}, u32[]{:S(2)}) copy-start(bf16[2,2,256,240]{3,2,1,0:T(8,128)(2,1)} %constant.13.clone.refs_6_) | copy-start | bytes 1474564
  8.6 6.6 %copy-start.5 = (bf16[2,2,240,256]{3,2,1,0:T(8,128)(2,1)S(1)}, bf16[2,2,240,256]{3,2,1,0:T(8,128)(2,1)}, u32[]{:S(2)}) copy-start(bf16[2,2,240,256]{3,2,1,0:T(8,128)(2,1)} %constant.12.clone.refs_5_) | copy-start | bytes 1474564
  8.6 6.6 %copy-start.6 = (bf16[2,128,480]{2,1,0:T(8,128)(2,1)S(1)}, bf16[2,128,480]{2,1,0:T(8,128)(2,1)}, u32[]{:S(2)}) copy-start(bf16[2,128,480]{2,1,0:T(8,128)(2,1)} %constant.14.clone.refs_7_) | copy-start | bytes 737284
  8.6 6.6 %copy-start.7 = (bf16[480,256]{1,0:T(8,128)(2,1)S(1)}, bf16[480,256]{1,0:T(8,128)(2,1)}, u32[]{:S(2)}) copy-start(bf16[480,256]{1,0:T(8,128)(2,1)} %constant.15.clone.refs_8_) | copy-start | bytes 737284
  10.3 5.0 %copy-start.3 = (f32[240,480]{1,0:T(8,128)S(1)}, f32[240,480]{1,0:T(8,128)}, u32[]{:S(2)}) copy-start(f32[240,480]{1,0:T(8,128)} %refs_3_.2) | copy-start | bytes 1382404
  10.6 4.5 %collective-permute-start.4 = (bf16[2,2,80,128]{3,2,1,0:T(8,128)(2,1)S(1)}, bf16[2,2,80,128]{3,2,1,0:T(8,128)(2,1)S(1)}, u32[]{:S(2)}, u32[]{:S(2)}) collective-permute-start(bf16[2,2,80,128]{3,2,1,0:T(8,128)(2,1)S(1)} %pad_maximum_fusion), channel_id=1, source_target_pairs={{0,4},{2,6},{4,0},{6,2},{8,12},{10,14},{12,8},{14,10},{16,20},{18,... | collective-permute-start | bytes 245768 | tf_op jit(solution)/shard_map/ppermute | solution.py:386
  15.1 7.0 %collective-permute-start.5 = (bf16[2,5,80,128]{3,2,1,0:T(8,128)(2,1)S(1)}, bf16[2,5,80,128]{3,2,1,0:T(8,128)(2,1)S(1)}, u32[]{:S(2)}, u32[]{:S(2)}) collective-permute-start(bf16[2,5,80,128]{3,2,1,0:T(8,128)(2,1)S(1)} %constant_dynamic-update-slice_fusion.refs_5_), channel_id=1, source_target_pairs={{0,2},{2,0},{4,6},{6,4},{8,10},{10,8},{12,14},{14,12},{16,18},{18,... | collective-permute-start | bytes 614408 | tf_op jit(solution)/shard_map/ppermute | solution.py:407
  17.2 4.9 %collective-permute-start.3 = (f32[80,256]{1,0:T(8,128)S(1)}, f32[80,256]{1,0:T(8,128)S(1)}, u32[]{:S(2)}, u32[]{:S(2)}) collective-permute-start(f32[80,256]{1,0:T(8,128)S(1)} %bitcast.10), channel_id=1, source_target_pairs={{0,1},{1,0},{2,3},{3,2},{4,5},{5,4},{6,7},{7,6},{8,9},{9,8},{10,11... | collective-permute-start | bytes 245768 | tf_op jit(solution)/shard_map/ppermute | solution.py:411

commit v2 on v1

--- a/solution.py
+++ b/solution.py
@@ -127,26 +127,45 @@
     return lax.rem(ga + (groups - distance), groups)
 
 
-def place_kernel(ga_ref, rows_ref, orbitals_ref, entries_ref, out_ref, inverse_ref, e_ref, all_ref):
+def place_kernel(
+    ga_ref, rows_ref, orbitals_ref, entries_ref, sticks_ref, out_ref, inverse_ref, in_ref, pick_ref, kinetic_ref, e_ref, all_ref
+):
     width = entries_ref.shape[1]
     slots = orbitals_ref.shape[2]
     total = entries_ref.shape[0]
     groups = total // slots
+    radius = width // 2
     ga = ga_ref[0]
     chunks, _, lanes = e_ref.shape
     lists_t = entries_ref[...].astype(F32)
-    if chunks * lanes > total:
-        lists_t = jnp.concatenate([lists_t, jnp.full((chunks * lanes - total, width), -1.0, F32)], axis=0)
     position = rows_ref[...]
     for chunk in range(chunks):
-        e_ref[chunk] = lists_t[chunk * lanes : (chunk + 1) * lanes].T
+        first = chunk * lanes
+        used = min(lanes, total - first)
+        copies = 1
+        while used * copies * 2 <= lanes and lanes % (used * copies * 2) == 0:
+            copies *= 2
+        if used * copies < lanes:
+            copies, used_rows = 1, jnp.concatenate([lists_t[first:], jnp.full((lanes - used, width), -1.0, F32)], axis=0)
+        else:
+            used_rows = jnp.concatenate([lists_t[first : first + used]] * copies, axis=0)
+        e_ref[chunk] = used_rows.T
+        height = width // copies
+        target = position[:height]
+        if copies > 1:
+            lane = lax.broadcasted_iota(jnp.int32, (height, lanes), 1).astype(F32)
+            for copy in range(1, copies):
+                target = jnp.where(lane >= copy * used, position[:height] + copy * height, target)
 
         def step(k, found):
-            match = e_ref[chunk, pl.ds(k, 1), :] == position
+            match = e_ref[chunk, pl.ds(k, 1), :] == target
             return jnp.where(match, k.astype(F32), found)
 
-        found = lax.fori_loop(0, width, step, jnp.full((width, lanes), -1.0, F32), unroll=8)
-        all_ref[chunk * lanes : (chunk + 1) * lanes, :] = found.T.astype(jnp.int32)
+        found = lax.fori_loop(0, width, step, jnp.full((height, lanes), -1.0, F32), unroll=8)
+        if copies > 1:
+            found = jnp.concatenate([found[:, c * used : (c + 1) * used] for c in range(copies)], axis=0)
+        found = found.T.astype(jnp.int32)
+        all_ref[first : first + found.shape[0], :] = found
 
     def lists(group):
         return all_ref[pl.ds(pl.multiple_of(group * slots, 8), slots), :]
@@ -154,20 +173,27 @@
     out_ref[...] = spread([orbitals_ref[0, 0], orbitals_ref[1, 0]], lists(ga))
     for distance in range(1, groups):
         inverse_ref[distance - 1] = lists(group_before(ga, distance, groups))
-
-
-def grid_kernel(ga_ref, other_refs, own_coeffs_ref, inverse_ref, potential_ref, sticks_ref, tables, own_ref, send_ref):
+    lane = lax.broadcasted_iota(jnp.int32, (slots, width), 1)
+    for distance in range(groups):
+        in_ref[distance] = choose_slots(sticks_ref, group_before(ga, distance, groups), slots, width)
+        row = canonical_lane(sticks_of(sticks_ref, lax.rem(ga + distance, groups), slots), radius).astype(F32)
+        column = jnp.broadcast_to(row, (width, slots)).T.astype(jnp.int32)
+        pick_ref[distance] = (column == lane).astype(F32).astype(BF16)
+    gx_row = (sticks_of(sticks_ref, ga, slots) - radius + 1).astype(F32)
+    gx = jnp.broadcast_to(gx_row, (width, slots)).T
+    gz = (entries_ref[pl.ds(pl.multiple_of(ga * slots, 8), slots), :] - radius + 1).astype(F32)
+    kinetic_ref[...] = (gx * gx + gz * gz) * (1.0 / (radius * radius))
+
+
+def grid_kernel(ga_ref, other_refs, own_coeffs_ref, inverse_ref, in_ref, pick_ref, potential_ref, tables, own_ref, send_ref):
     z_table, zt_table, x_table, xt = tables
     planes, _ = potential_ref.shape
     width = own_coeffs_ref.shape[1] // 2
     radius = width // 2
-    slots = own_ref.shape[0]
-    groups = sticks_ref.shape[1] // slots
     ga = ga_ref[0]
-    coeffs = dot(choose_slots(sticks_ref, ga, slots, width), own_coeffs_ref[...])
+    coeffs = dot(in_ref[0], own_coeffs_ref[...])
     for distance, ref in enumerate(other_refs, 1):
-        choose = choose_slots(sticks_ref, group_before(ga, distance, groups), slots, width)
-        coeffs = coeffs + dot(choose, spread([ref[0, 0], ref[1, 0]], inverse_ref[distance - 1]))
+        coeffs = coeffs + dot(in_ref[distance], spread([ref[0, 0], ref[1, 0]], inverse_ref[distance - 1]))
     real_part, imag_part = coeffs[:, :width], coeffs[:, width:]
     rows = jnp.concatenate(
         [
@@ -217,12 +243,8 @@
     )
     spec_high, spec_low = split(spectra)
     spec = jnp.concatenate([spec_high, spec_low], axis=1)
-    lanes = lax.broadcasted_iota(jnp.int32, (slots, width), 1)
-    for distance in range(groups):
-        group = lax.rem(ga + distance, groups)
-        lane_row = canonical_lane(sticks_of(sticks_ref, group, slots), radius).astype(F32)
-        lane_col = jnp.broadcast_to(lane_row, (width, slots)).T.astype(jnp.int32)
-        choose = (lane_col == lanes).astype(F32).astype(BF16)
+    for distance in range(pick_ref.shape[0]):
+        choose = pick_ref[distance]
         picked = dot_rows(jnp.concatenate([choose, choose], axis=1), spec)
         if distance == 0:
             own_ref[...] = picked
@@ -230,20 +252,16 @@
             send_ref[distance - 1] = picked
 
 
-def apply_part(ga, partial_refs, orbitals_ref, entries_ref, sticks_ref, points):
+def apply_part(ga, partial_refs, orbitals_ref, entries_ref, kinetic_ref, points):
     width = entries_ref.shape[1]
     slots = orbitals_ref.shape[2]
-    radius = width // 2
     total = partial_refs[0][...]
     for ref in partial_refs[1:]:
         total = total + ref[...]
     entries = entries_ref[pl.ds(pl.multiple_of(ga * slots, 8), slots), :]
     present = entries >= 0
     index = jnp.maximum(entries, 0)
-    gx_row = (sticks_of(sticks_ref, ga, entries.shape[0]) - radius + 1).astype(F32)
-    gx = jnp.broadcast_to(gx_row, (width, gx_row.shape[1])).T
-    gz = (entries - radius + 1).astype(F32)
-    kinetic = (gx * gx + gz * gz) * (1.0 / (radius * radius))
+    kinetic = kinetic_ref[...]
     result = []
     for part in range(2):
         picked = jnp.take_along_axis(
@@ -254,9 +272,9 @@
     return result, present
 
 
-def final_kernel(points, ga_ref, partial_refs, orbitals_ref, entries_ref, sticks_ref, psi_refs, out_ref, sums_ref):
+def final_kernel(points, ga_ref, partial_refs, orbitals_ref, entries_ref, kinetic_ref, psi_refs, out_ref, sums_ref):
     ga = ga_ref[0]
-    result, present = apply_part(ga, partial_refs, orbitals_ref, entries_ref, sticks_ref, points)
+    result, present = apply_part(ga, partial_refs, orbitals_ref, entries_ref, kinetic_ref, points)
     for part in range(2):
         out_ref[part, 0] = result[part]
     _, width = present.shape
@@ -369,17 +387,20 @@
         out_shape=(
             jax.ShapeDtypeStruct((slots, 2 * width), BF16),
             jax.ShapeDtypeStruct((groups - 1, slots, width), jnp.int32),
+            jax.ShapeDtypeStruct((groups, width, slots), BF16),
+            jax.ShapeDtypeStruct((groups, slots, width), BF16),
+            jax.ShapeDtypeStruct((slots, width), F32),
         ),
-        in_specs=[SMEM_SPEC] + [VMEM_SPEC] * 3,
-        out_specs=(VMEM_SPEC, VMEM_SPEC),
+        in_specs=[SMEM_SPEC] + [VMEM_SPEC] * 4,
+        out_specs=(VMEM_SPEC,) * 5,
         scratch_shapes=[pltpu.VMEM((chunks, width, 128), F32), pltpu.VMEM((chunks * 128, width), jnp.int32)],
         compiler_params=KERNEL_PARAMS,
         cost_estimate=pl.CostEstimate(flops=SPREAD_FLOPS, bytes_accessed=0, transcendentals=0),
         name="place",
     )
-    coeffs, inverse = place(ga, rows, orbitals, stick_entries)
-    coeffs, *arrived = lax.optimization_barrier((coeffs, *near, *far))
-    near, far = jnp.concatenate(arrived[: len(near)], axis=1), arrived[len(near) :]
+    coeffs, inverse, into, pick, kinetic = place(ga, rows, orbitals, stick_entries, sticks)
+    coeffs, *near = lax.optimization_barrier((coeffs, *near))
+    near = jnp.concatenate(near, axis=1)
     psi = [near]
     if layout.ny == 2:
         pairs = [(i, i ^ layout.nc) for i in range(band_total)]
@@ -387,7 +408,7 @@
 
     def run_grid(ga_ref, *refs):
         count = len(others)
-        grid_kernel(ga_ref, refs[:count], *refs[count : count + 4], refs[count + 4 : count + 8], *refs[count + 8 :])
+        grid_kernel(ga_ref, refs[:count], *refs[count : count + 5], refs[count + 5 : count + 9], *refs[count + 9 :])
 
     grid = pl.pallas_call(
         run_grid,
@@ -395,13 +416,14 @@
             jax.ShapeDtypeStruct((slots, 2 * width), F32),
             jax.ShapeDtypeStruct((groups - 1, slots, 2 * width), F32),
         ),
-        in_specs=[SMEM_SPEC] + [VMEM_SPEC] * (len(others) + 8),
+        in_specs=[SMEM_SPEC] + [VMEM_SPEC] * (len(others) + 9),
         out_specs=(VMEM_SPEC, VMEM_SPEC),
         compiler_params=KERNEL_PARAMS,
         cost_estimate=pl.CostEstimate(flops=GRID_FLOPS, bytes_accessed=0, transcendentals=0),
         name="grid",
     )
-    own, send = grid(ga, *others, coeffs, inverse, potential, sticks, *tables)
+    own, send = grid(ga, *others, coeffs, inverse, into, pick, potential, *tables)
+    own, *far = lax.optimization_barrier((own, *far))
     psi = [jnp.concatenate(psi + far, axis=1)]
     if layout.nc == 2:
         psi.append(lax.ppermute(psi[0], "band", [(i, i ^ 1) for i in range(band_total)]))
@@ -428,7 +450,7 @@
             out_specs=VMEM_SPEC,
             compiler_params=KERNEL_PARAMS,
             name="apply",
-        )(ga, *partials, orbitals, stick_entries, sticks)
+        )(ga, *partials, orbitals, stick_entries, kinetic)
         own_lists = lax.dynamic_slice_in_dim(stick_entries, ga[0] * slots, slots, 0)
         masked = jnp.where(own_lists >= 0, orbitals, jnp.zeros_like(orbitals))
         correlation, reduced = general_matrices(jnp.stack(psi, axis=2), masked, applied, layout, scale)
@@ -445,7 +467,7 @@
         out_specs=(VMEM_SPEC, VMEM_SPEC),
         compiler_params=KERNEL_PARAMS,
         name="final",
-    )(ga, *partials, orbitals, stick_entries, sticks, *psi)
+    )(ga, *partials, orbitals, stick_entries, kinetic, *psi)
     everywhere = lax.all_to_all(sums, ("ga", "band"), split_axis=0, concat_axis=0, tiled=True)
     matrix = jax.ShapeDtypeStruct((2, band_total, band_total), F32)
 

time: 34.6 us -> 31.4 us (0.908)
  waiting for transfers between devices: 6.73 us -> 5.24 us
  starting transfers between devices: 10.1 us -> 9.39 us
  blocking collectives: 10.7 us -> 10.1 us
  Pallas kernels: 5.27 us -> 4.85 us
    ppermute x1, waiting for transfers between devices: 3.13 us -> 0.99 us  [body(): psi.append(lax.ppermute(near, 'band', pairs))]
    ppermute x1, starting transfers between devices: 1.56 us -> 0.6 us  [body(): partials.append(lax.ppermute(send[distance - 1], 'ga', pairs))]
    ppermute x1, waiting for transfers between devices: 3.33 us -> 4.25 us  [body(): partials.append(lax.ppermute(send[distance - 1], 'ga', pairs))]
    all_to_all x1, blocking collectives: 10.7 us -> 10.1 us  [body(): lax.all_to_all(sums, ('ga', 'band'), split_axis=0, concat_axis=0, tiled=T...]
  transfers between devices with their start and end apart: 6 -> 6, of which waited for: 3 -> 2; matrix products, arithmetic and copies ran while one was open for 0% -> 0% of each run, Pallas kernels for 10% -> 11%
where the time goes in v2:
time: 31.4 us; the launch traced here: 31.3 us
  blocking collectives  10.1 us (32%)
  starting transfers between devices  9.39 us (30%)
  waiting for transfers between devices  5.24 us (17%)
  Pallas kernels  4.85 us (15%)
  local copies, waits for them, and re-layouts  0.86 us (3%)
  between operations  0.78 us (2%)
    all_to_all x1, blocking collectives, body(): lax.all_to_all(sums, ('ga', 'band'), split_axis=0, concat_axis=0, tiled=T...  10.1 us
    ppermute x2, starting transfers between devices, body(): lax.ppermute(orbitals, 'band', layout.pairs(part))  5.64 us
    ppermute x1, waiting for transfers between devices, body(): partials.append(lax.ppermute(send[distance - 1], 'ga', pairs))  4.25 us
    pallas_call x1, Pallas kernels, body(): grid(ga, *others, coeffs, inverse, into, pick, potential, *tables)  1.86 us
    ppermute x1, starting transfers between devices, body(): psi.append(lax.ppermute(near, 'band', pairs))  1.58 us
    ppermute x1, starting transfers between devices, body(): others.append(lax.ppermute(orbitals, 'ga', pairs))  1.49 us
    pallas_call x1, Pallas kernels, body(): place(ga, rows, orbitals, stick_entries, sticks)  1.43 us
    ppermute x1, waiting for transfers between devices, body(): psi.append(lax.ppermute(near, 'band', pairs))  0.99 us
  transfers between devices with their start and end apart: 6, of which 2 were waited for; matrix products, arithmetic and copies ran while one was open for 0% of the time, Pallas kernels for 11%

profile of v2, /device:TPU:0, one launch (start us, length us, event | category | flops | bytes accessed | tf_op | source)
XLA Modules:
  0.0 31.3 jit_solution(6696137325361074763)
XLA Ops:
  0.6 0.0 copy-start.1
  0.6 0.0 copy-start.2
  0.7 0.0 copy-start
  0.7 0.7 %copy-done.2 = s32[160]{0:T(256)S(1)} copy-done((s32[160]{0:T(256)S(1)}, s32[160]{0:T(256)}, u32[]{:S(2)}) %copy-start.2) | copy-done | bytes 664
  1.4 0.1 copy-done
  1.5 3.1 %collective-permute-start.1 = (bf16[2,1,80,128]{3,2,1,0:T(8,128)(2,1)S(1)}, bf16[2,1,80,128]{3,2,1,0:T(8,128)(2,1)S(1)}, u32[]{:S(2)}, u32[]{:S(2)}) collective-permute-start(bf16[2,1,80,128]{3,2,1,0:T(8,128)(2,1)S(1)} %copy-done), channel_id=1, source_target_pairs={{24,0},{26,2},{28,4},{30,6},{0,8},{2,10},{4,12},{6,14},{8,16},{10,... | collective-permute-start | bytes 122888 | tf_op jit(solution)/shard_map/ppermute | solution.py:382
  4.5 1.5 %collective-permute-start = (bf16[2,1,80,128]{3,2,1,0:T(8,128)(2,1)S(1)}, bf16[2,1,80,128]{3,2,1,0:T(8,128)(2,1)S(1)}, u32[]{:S(2)}, u32[]{:S(2)}) collective-permute-start(bf16[2,1,80,128]{3,2,1,0:T(8,128)(2,1)S(1)} %copy-done), channel_id=1, source_target_pairs={{0,1},{1,0},{2,3},{3,2},{4,5},{5,4},{6,7},{7,6},{8,9},{9,8},{10,11... | collective-permute-start | bytes 122888 | tf_op jit(solution)/shard_map/ppermute | solution.py:378
  6.0 2.6 %collective-permute-start.2 = (bf16[2,1,80,128]{3,2,1,0:T(8,128)(2,1)S(1)}, bf16[2,1,80,128]{3,2,1,0:T(8,128)(2,1)S(1)}, u32[]{:S(2)}, u32[]{:S(2)}) collective-permute-start(bf16[2,1,80,128]{3,2,1,0:T(8,128)(2,1)S(1)} %copy-done), channel_id=1, source_target_pairs={{20,0},{22,2},{16,4},{18,6},{28,8},{30,10},{24,12},{26,14},{0,16},... | collective-permute-start | bytes 122888 | tf_op jit(solution)/shard_map/ppermute | solution.py:382
  8.6 0.0 copy-start.6
  8.6 1.4 %place.1 = (bf16[80,256]{1,0:T(8,128)(2,1)S(1)}, s32[1,80,128]{2,1,0:T(8,128)S(1)}, bf16[2,128,80]{2,1,0:T(8,128)(2,1)S(1)}, bf16[2,80,128]{2,1,0:T(8,128)(2,1)S(1)}, f32[80,128]{1,0:T(8,128)S(1)}) custom-call(s32[1]{0:T(128)} %bitcast.ga_ref, f32[128,128]{1,0:T(8,128)S(1)} %rows.1._.rows_ref, bf16[2,1,80,128]{3,2,1,0:T(8,128)(2,1)S(1)} %copy-done, ...), custom_call_target="tpu_custom_call" | custom-call | flops 1500000000 | tf_op jit(solution)/shard_map/place/pallas_call | solution.py:401
  10.1 0.0 copy-start.7
  10.1 0.0 collective-permute-done.1
  10.1 1.6 %collective-permute-start.4 = (bf16[2,2,80,128]{3,2,1,0:T(8,128)(2,1)S(1)}, bf16[2,2,80,128]{3,2,1,0:T(8,128)(2,1)S(1)}, u32[]{:S(2)}, u32[]{:S(2)}) collective-permute-start(bf16[2,2,80,128]{3,2,1,0:T(8,128)(2,1)S(1)} %pad_maximum_fusion), channel_id=1, source_target_pairs={{0,4},{2,6},{4,0},{6,2},{8,12},{10,14},{12,8},{14,10},{16,20},{18,... | collective-permute-start | bytes 245768 | tf_op jit(solution)/shard_map/ppermute | solution.py:407
  11.7 0.0 collective-permute-done.refs_0_
  11.7 1.9 %grid.1 = (f32[80,256]{1,0:T(8,128)S(1)}, f32[1,80,256]{2,1,0:T(8,128)S(1)}) custom-call(s32[1]{0:T(128)} %bitcast.ga_ref, bf16[2,1,80,128]{3,2,1,0:T(8,128)(2,1)S(1)} %collective-permute-done.refs_0_, bf16[80,256]{1,0:T(8,128)(2,1)S(1)} %get-tuple-element.26.refs_1_, s32[1,80,128]{2,1,0:T(8,128)S(1)} %get-tuple-element.27.refs_2_, ...), custom_call_target="tpu_custom_call" | custom-call | flops 3000000000 | tf_op jit(solution)/shard_map/grid/pallas_call | solution.py:425
  13.6 0.0 collective-permute-done.2
  13.6 1.0 %collective-permute-done.4 = bf16[2,2,80,128]{3,2,1,0:T(8,128)(2,1)S(1)} collective-permute-done((bf16[2,2,80,128]{3,2,1,0:T(8,128)(2,1)S(1)}, bf16[2,2,80,128]{3,2,1,0:T(8,128)(2,1)S(1)}, u32[]{:S(2)}, u32[]{:S(2)}) %collective-permute-start.4) | collective-permute-done | bytes 81952 | tf_op jit(solution)/shard_map/ppermute | solution.py:407
  14.7 0.1 collective-permute-start.5
  14.7 0.6 %collective-permute-start.3 = (f32[80,256]{1,0:T(8,128)S(1)}, f32[80,256]{1,0:T(8,128)S(1)}, u32[]{:S(2)}, u32[]{:S(2)}) collective-permute-start(f32[80,256]{1,0:T(8,128)S(1)} %bitcast.10), channel_id=1, source_target_pairs={{0,1},{1,0},{2,3},{3,2},{4,5},{5,4},{6,7},{7,6},{8,9},{9,8},{10,11... | collective-permute-start | bytes 245768 | tf_op jit(solution)/shard_map/ppermute | solution.py:433
  15.3 4.2 %collective-permute-done.3.refs_1_ = f32[80,256]{1,0:T(8,128)S(1)} collective-permute-done((f32[80,256]{1,0:T(8,128)S(1)}, f32[80,256]{1,0:T(8,128)S(1)}, u32[]{:S(2)}, u32[]{:S(2)}) %collective-permute-start.3) | collective-permute-done | bytes 81952 | tf_op jit(solution)/shard_map/ppermute | solution.py:433
  19.6 0.0 collective-permute-done.5.refs_6_
  19.6 0.8 %final.1 = (bf16[2,1,80,128]{3,2,1,0:T(8,128)(2,1)}, f32[32,128]{1,0:T(8,128)S(1)}) custom-call(s32[1]{0:T(128)} %bitcast.ga_ref, f32[80,256]{1,0:T(8,128)S(1)} %get-tuple-element.31.refs_0_, f32[80,256]{1,0:T(8,128)S(1)} %collective-permute-done.3.refs_1_, bf16[2,1,80,128]{3,2,1,0:T(8,128)(2,1)S(1)} %copy-done, s32[160,128]{1,0:T(8,128)S(1)} %copy-done.1, ...), custom_call_target="tpu_custom_call" | custom-call | tf_op jit(solution)/shard_map/final/pallas_call | solution.py:463
  20.4 10.1 %all_to_all.11 = f32[32,1,128]{2,1,0:T(1,128)S(1)} all-to-all(f32[32,1,128]{2,1,0:T(1,128)S(1)} %bitcast.8), channel_id=1, replica_groups=mesh['band'=16,'ga'=2] {'ga','band'}, dimensions={0} | all-to-all | bytes 32768 | tf_op jit(solution)/shard_map/all_to_all | solution.py:471
  30.5 0.8 %assemble.1 = (f32[2,16,16]{2,1,0:T(8,128)}, f32[2,16,16]{2,1,0:T(8,128)}) custom-call(f32[32,128]{1,0:T(8,128)S(1)} %bitcast.7), custom_call_target="tpu_custom_call" | custom-call | tf_op jit(solution)/shard_map/assemble/pallas_call | solution.py:477
  (16 shorter events, 0.1 us)
Async XLA Ops:
  0.6 8.0 %copy-start.1 = (s32[160,128]{1,0:T(8,128)S(1)}, s32[160,128]{1,0:T(8,128)}, u32[]{:S(2)}) copy-start(s32[160,128]{1,0:T(8,128)} %refs_3_.1) | copy-start | bytes 245764
  0.6 0.7 %copy-start.2 = (s32[160]{0:T(256)S(1)}, s32[160]{0:T(256)}, u32[]{:S(2)}) copy-start(s32[160]{0:T(256)} %param.10) | copy-start | bytes 1924
  0.7 0.8 %copy-start = (bf16[2,1,80,128]{3,2,1,0:T(8,128)(2,1)S(1)}, bf16[2,1,80,128]{3,2,1,0:T(8,128)(2,1)}, u32[]{:S(2)}) copy-start(bf16[2,1,80,128]{3,2,1,0:T(8,128)(2,1)} %refs_2_) | copy-start | bytes 122884
  1.5 8.6 %collective-permute-start.1 = (bf16[2,1,80,128]{3,2,1,0:T(8,128)(2,1)S(1)}, bf16[2,1,80,128]{3,2,1,0:T(8,128)(2,1)S(1)}, u32[]{:S(2)}, u32[]{:S(2)}) collective-permute-start(bf16[2,1,80,128]{3,2,1,0:T(8,128)(2,1)S(1)} %copy-done), channel_id=1, source_target_pairs={{24,0},{26,2},{28,4},{30,6},{0,8},{2,10},{4,12},{6,14},{8,16},{10,... | collective-permute-start | bytes 122888 | tf_op jit(solution)/shard_map/ppermute | solution.py:382
  4.5 7.2 %collective-permute-start = (bf16[2,1,80,128]{3,2,1,0:T(8,128)(2,1)S(1)}, bf16[2,1,80,128]{3,2,1,0:T(8,128)(2,1)S(1)}, u32[]{:S(2)}, u32[]{:S(2)}) collective-permute-start(bf16[2,1,80,128]{3,2,1,0:T(8,128)(2,1)S(1)} %copy-done), channel_id=1, source_target_pairs={{0,1},{1,0},{2,3},{3,2},{4,5},{5,4},{6,7},{7,6},{8,9},{9,8},{10,11... | collective-permute-start | bytes 122888 | tf_op jit(solution)/shard_map/ppermute | solution.py:378
  6.0 7.6 %collective-permute-start.2 = (bf16[2,1,80,128]{3,2,1,0:T(8,128)(2,1)S(1)}, bf16[2,1,80,128]{3,2,1,0:T(8,128)(2,1)S(1)}, u32[]{:S(2)}, u32[]{:S(2)}) collective-permute-start(bf16[2,1,80,128]{3,2,1,0:T(8,128)(2,1)S(1)} %copy-done), channel_id=1, source_target_pairs={{20,0},{22,2},{16,4},{18,6},{28,8},{30,10},{24,12},{26,14},{0,16},... | collective-permute-start | bytes 122888 | tf_op jit(solution)/shard_map/ppermute | solution.py:382
  8.6 3.1 %copy-start.3 = (f32[240,480]{1,0:T(8,128)S(1)}, f32[240,480]{1,0:T(8,128)}, u32[]{:S(2)}) copy-start(f32[240,480]{1,0:T(8,128)} %refs_5_.1) | copy-start | bytes 1382404
  8.6 3.1 %copy-start.4 = (bf16[2,2,256,240]{3,2,1,0:T(8,128)(2,1)S(1)}, bf16[2,2,256,240]{3,2,1,0:T(8,128)(2,1)}, u32[]{:S(2)}) copy-start(bf16[2,2,256,240]{3,2,1,0:T(8,128)(2,1)} %constant.13.clone.refs_7_) | copy-start | bytes 1474564
  8.6 3.1 %copy-start.5 = (bf16[2,2,240,256]{3,2,1,0:T(8,128)(2,1)S(1)}, bf16[2,2,240,256]{3,2,1,0:T(8,128)(2,1)}, u32[]{:S(2)}) copy-start(bf16[2,2,240,256]{3,2,1,0:T(8,128)(2,1)} %constant.12.clone.refs_6_) | copy-start | bytes 1474564
  8.6 3.1 %copy-start.6 = (bf16[2,128,480]{2,1,0:T(8,128)(2,1)S(1)}, bf16[2,128,480]{2,1,0:T(8,128)(2,1)}, u32[]{:S(2)}) copy-start(bf16[2,128,480]{2,1,0:T(8,128)(2,1)} %constant.14.clone.refs_8_) | copy-start | bytes 737284
  10.1 1.7 %copy-start.7 = (bf16[480,256]{1,0:T(8,128)(2,1)S(1)}, bf16[480,256]{1,0:T(8,128)(2,1)}, u32[]{:S(2)}) copy-start(bf16[480,256]{1,0:T(8,128)(2,1)} %constant.15.clone.refs_9_) | copy-start | bytes 737284
  10.1 4.5 %collective-permute-start.4 = (bf16[2,2,80,128]{3,2,1,0:T(8,128)(2,1)S(1)}, bf16[2,2,80,128]{3,2,1,0:T(8,128)(2,1)S(1)}, u32[]{:S(2)}, u32[]{:S(2)}) collective-permute-start(bf16[2,2,80,128]{3,2,1,0:T(8,128)(2,1)S(1)} %pad_maximum_fusion), channel_id=1, source_target_pairs={{0,4},{2,6},{4,0},{6,2},{8,12},{10,14},{12,8},{14,10},{16,20},{18,... | collective-permute-start | bytes 245768 | tf_op jit(solution)/shard_map/ppermute | solution.py:407
  14.7 4.9 %collective-permute-start.5 = (bf16[2,5,80,128]{3,2,1,0:T(8,128)(2,1)S(1)}, bf16[2,5,80,128]{3,2,1,0:T(8,128)(2,1)S(1)}, u32[]{:S(2)}, u32[]{:S(2)}) collective-permute-start(bf16[2,5,80,128]{3,2,1,0:T(8,128)(2,1)S(1)} %constant_dynamic-update-slice_fusion.refs_5_), channel_id=1, source_target_pairs={{0,2},{2,0},{4,6},{6,4},{8,10},{10,8},{12,14},{14,12},{16,18},{18,... | collective-permute-start | bytes 614408 | tf_op jit(solution)/shard_map/ppermute | solution.py:429
  14.7 4.8 %collective-permute-start.3 = (f32[80,256]{1,0:T(8,128)S(1)}, f32[80,256]{1,0:T(8,128)S(1)}, u32[]{:S(2)}, u32[]{:S(2)}) collective-permute-start(f32[80,256]{1,0:T(8,128)S(1)} %bitcast.10), channel_id=1, source_target_pairs={{0,1},{1,0},{2,3},{3,2},{4,5},{5,4},{6,7},{7,6},{8,9},{9,8},{10,11... | collective-permute-start | bytes 245768 | tf_op jit(solution)/shard_map/ppermute | solution.py:433

commit v3 on v2

--- a/solution.py
+++ b/solution.py
@@ -43,7 +43,7 @@
     zt_high, zt_low = hi_lo_table(backward)
     x_high, x_low = hi_lo_table(x_table)
     xt = np.concatenate([x_high.T, x_low.T], axis=1)
-    return np.stack([z_high, z_low], 1), np.stack([zt_high, zt_low], 1), np.stack([x_high, x_low]), xt
+    return np.concatenate([z_high, z_low], 1), np.stack([zt_high, zt_low], 1), np.stack([x_high, x_low]), xt
 
 
 def split(values):
@@ -77,7 +77,7 @@
         block = device // self.inner if where is np.where else lax.div(device, self.inner)
         place = device - block * self.inner
         if self.parts[part] is None:
-            turned = where(block < self.half, self.ny - 1, 0)
+            turned = where(block < self.half, 0, self.ny - 1)
             block = where(block < self.half, block + self.half, block - self.half)
         else:
             shift, turned = self.parts[part]
@@ -202,7 +202,8 @@
         ],
         axis=0,
     ).astype(BF16)
-    columns = dot_rows(z_table[ga, 0], rows) + dot_rows(z_table[ga, 1], rows)
+    columns = dot_rows(z_table[ga], rows)
+    columns = columns[:planes] + columns[planes:]
     col_re, col_im = columns[:, :width], columns[:, width:]
     rol_re, rol_im = pltpu.roll(col_re, radius, 1), pltpu.roll(col_im, radius, 1)
     even = lax.broadcasted_iota(jnp.int32, (planes, width), 1) < radius
@@ -297,7 +298,8 @@
     sums_ref[...] = jnp.broadcast_to(sums, sums_ref.shape)
 
 
-def assemble_kernel(groups, layout, scale, sums_ref, corr_ref, ham_ref):
+def assemble_kernel(groups, layout, scale, sums_ref, applied_ref, out_ref, corr_ref, ham_ref):
+    out_ref[...] = applied_ref[...]
     bands = layout.total
     total = sums_ref[0:bands, :]
     for group in range(1, groups):
@@ -371,7 +373,6 @@
         compiler_params=KERNEL_PARAMS,
         name="sticks",
     )(rows, sticks)
-    orbitals, rows, sticks = lax.optimization_barrier((orbitals, rows, sticks))
     others = []
     for distance in range(1, groups):
         pairs = [(i, (i + distance) % groups) for i in range(groups)]
@@ -471,17 +472,14 @@
     everywhere = lax.all_to_all(sums, ("ga", "band"), split_axis=0, concat_axis=0, tiled=True)
     matrix = jax.ShapeDtypeStruct((2, band_total, band_total), F32)
 
-    def run_assemble(sums_ref, corr_ref, ham_ref):
-        assemble_kernel(groups, layout, scale, sums_ref, corr_ref, ham_ref)
-
-    correlation, reduced = pl.pallas_call(
-        run_assemble,
-        out_shape=(matrix, matrix),
-        in_specs=[VMEM_SPEC],
-        out_specs=(VMEM_SPEC, VMEM_SPEC),
+    applied, correlation, reduced = pl.pallas_call(
+        functools.partial(assemble_kernel, groups, layout, scale),
+        out_shape=(out_type, matrix, matrix),
+        in_specs=[VMEM_SPEC, VMEM_SPEC],
+        out_specs=(VMEM_SPEC,) * 3,
         compiler_params=KERNEL_PARAMS,
         name="assemble",
-    )(everywhere)
+    )(everywhere, applied)
     return applied, correlation, reduced
 
 

time: 31.4 us -> 30.9 us (0.984)
  blocking collectives: 10.1 us -> 8.87 us
  waiting for transfers between devices: 5.24 us -> 5.99 us
  local copies, waits for them, and re-layouts: 0.86 us -> 1.23 us
  Pallas kernels: 4.85 us -> 4.48 us
    all_to_all x1, blocking collectives: 10.1 us -> 8.87 us  [body(): lax.all_to_all(sums, ('ga', 'band'), split_axis=0, concat_axis=0, tiled=T...]
    ppermute x1, starting transfers between devices: 1.58 us -> 0.57 us  [body(): psi.append(lax.ppermute(near, 'band', pairs))]
    ppermute x2, starting transfers between devices: 5.64 us -> 6.65 us  [body(): lax.ppermute(orbitals, 'band', layout.pairs(part))]
    ppermute x1, waiting for transfers between devices: 0.99 us -> 1.73 us  [body(): psi.append(lax.ppermute(near, 'band', pairs))]
    unnamed x19, local copies, waits for them, and re-layouts: 0.85 us -> 1.22 us
    pallas_call x1, Pallas kernels: 0.79 us -> 0.43 us  [body(): pl.pallas_call(run_final, out_shape=(out_type, jax.ShapeDtypeStruct((grou...]
where the time goes in v3:
time: 30.9 us; the launch traced here: 30.7 us
  starting transfers between devices  9.38 us (30%)
  blocking collectives  8.87 us (29%)
  waiting for transfers between devices  5.99 us (19%)
  Pallas kernels  4.48 us (14%)
  local copies, waits for them, and re-layouts  1.23 us (4%)
  between operations  0.76 us (2%)
    all_to_all x1, blocking collectives, body(): lax.all_to_all(sums, ('ga', 'band'), split_axis=0, concat_axis=0, tiled=T...  8.87 us
    ppermute x2, starting transfers between devices, body(): lax.ppermute(orbitals, 'band', layout.pairs(part))  6.65 us
    ppermute x1, waiting for transfers between devices, body(): partials.append(lax.ppermute(send[distance - 1], 'ga', pairs))  4.25 us
    pallas_call x1, Pallas kernels, body(): grid(ga, *others, coeffs, inverse, into, pick, potential, *tables)  1.85 us
    ppermute x1, waiting for transfers between devices, body(): psi.append(lax.ppermute(near, 'band', pairs))  1.73 us
    ppermute x1, starting transfers between devices, body(): others.append(lax.ppermute(orbitals, 'ga', pairs))  1.49 us
    pallas_call x1, Pallas kernels, body(): place(ga, rows, orbitals, stick_entries, sticks)  1.43 us
    unnamed x19, local copies, waits for them, and re-layouts  1.22 us
  transfers between devices with their start and end apart: 6, of which 2 were waited for; matrix products, arithmetic and copies ran while one was open for 0% of the time, Pallas kernels for 11%

profile of v3, /device:TPU:0, one launch (start us, length us, event | category | flops | bytes accessed | tf_op | source)
XLA Modules:
  0.0 30.7 jit_solution(2606642561461650201)
XLA Ops:
  0.6 3.1 %collective-permute-start.1 = (bf16[2,1,80,128]{3,2,1,0:T(8,128)(2,1)}, bf16[2,1,80,128]{3,2,1,0:T(8,128)(2,1)S(1)}, u32[]{:S(2)}, u32[]{:S(2)}) collective-permute-start(bf16[2,1,80,128]{3,2,1,0:T(8,128)(2,1)} %refs_2_.1), channel_id=1, source_target_pairs={{24,0},{26,2},{28,4},{30,6},{0,8},{2,10},{4,12},{6,14},{8,16},{10,... | collective-permute-start | bytes 122888 | tf_op jit(solution)/shard_map/ppermute | solution.py:383
  3.7 1.5 %collective-permute-start = (bf16[2,1,80,128]{3,2,1,0:T(8,128)(2,1)}, bf16[2,1,80,128]{3,2,1,0:T(8,128)(2,1)S(1)}, u32[]{:S(2)}, u32[]{:S(2)}) collective-permute-start(bf16[2,1,80,128]{3,2,1,0:T(8,128)(2,1)} %refs_2_.1), channel_id=1, source_target_pairs={{0,1},{1,0},{2,3},{3,2},{4,5},{5,4},{6,7},{7,6},{8,9},{9,8},{10,11... | collective-permute-start | bytes 122888 | tf_op jit(solution)/shard_map/ppermute | solution.py:379
  5.2 3.5 %collective-permute-start.2 = (bf16[2,1,80,128]{3,2,1,0:T(8,128)(2,1)}, bf16[2,1,80,128]{3,2,1,0:T(8,128)(2,1)S(1)}, u32[]{:S(2)}, u32[]{:S(2)}) collective-permute-start(bf16[2,1,80,128]{3,2,1,0:T(8,128)(2,1)} %refs_2_.1), channel_id=1, source_target_pairs={{16,0},{18,2},{20,4},{22,6},{24,8},{26,10},{28,12},{30,14},{4,16},... | collective-permute-start | bytes 122888 | tf_op jit(solution)/shard_map/ppermute | solution.py:383
  8.8 0.0 copy-start
  8.8 0.6 %copy-done.2 = s32[160]{0:T(256)S(1)} copy-done((s32[160]{0:T(256)S(1)}, s32[160]{0:T(256)}, u32[]{:S(2)}) %copy-start.2) | copy-done | bytes 664
  9.5 0.2 copy-done.1
  9.7 0.0 copy-done
  9.7 0.0 copy-start.6
  9.7 1.4 %place.1 = (bf16[80,256]{1,0:T(8,128)(2,1)S(1)}, s32[1,80,128]{2,1,0:T(8,128)S(1)}, bf16[2,128,80]{2,1,0:T(8,128)(2,1)S(1)}, bf16[2,80,128]{2,1,0:T(8,128)(2,1)S(1)}, f32[80,128]{1,0:T(8,128)S(1)}) custom-call(s32[1]{0:T(128)} %bitcast.ga_ref, f32[128,128]{1,0:T(8,128)S(1)} %rows.1._.rows_ref, bf16[2,1,80,128]{3,2,1,0:T(8,128)(2,1)S(1)} %copy-done, ...), custom_call_target="tpu_custom_call" | custom-call | flops 1500000000 | tf_op jit(solution)/shard_map/place/pallas_call | solution.py:402
  11.1 0.0 copy-start.7
  11.1 0.0 collective-permute-done.1
  11.2 0.6 %collective-permute-start.4 = (bf16[2,2,80,128]{3,2,1,0:T(8,128)(2,1)S(1)}, bf16[2,2,80,128]{3,2,1,0:T(8,128)(2,1)S(1)}, u32[]{:S(2)}, u32[]{:S(2)}) collective-permute-start(bf16[2,2,80,128]{3,2,1,0:T(8,128)(2,1)S(1)} %pad_maximum_fusion), channel_id=1, source_target_pairs={{0,4},{2,6},{4,0},{6,2},{8,12},{10,14},{12,8},{14,10},{16,20},{18,... | collective-permute-start | bytes 245768 | tf_op jit(solution)/shard_map/ppermute | solution.py:408
  11.8 0.0 collective-permute-done.refs_0_
  11.8 0.3 copy-done.7
  12.1 1.8 %grid.1 = (f32[80,256]{1,0:T(8,128)S(1)}, f32[1,80,256]{2,1,0:T(8,128)S(1)}) custom-call(s32[1]{0:T(128)} %bitcast.ga_ref, bf16[2,1,80,128]{3,2,1,0:T(8,128)(2,1)S(1)} %collective-permute-done.refs_0_, bf16[80,256]{1,0:T(8,128)(2,1)S(1)} %get-tuple-element.18.refs_1_, s32[1,80,128]{2,1,0:T(8,128)S(1)} %get-tuple-element.19.refs_2_, ...), custom_call_target="tpu_custom_call" | custom-call | flops 3000000000 | tf_op jit(solution)/shard_map/grid/pallas_call | solution.py:426
  13.9 0.0 collective-permute-done.2
  14.0 1.7 %collective-permute-done.4 = bf16[2,2,80,128]{3,2,1,0:T(8,128)(2,1)S(1)} collective-permute-done((bf16[2,2,80,128]{3,2,1,0:T(8,128)(2,1)S(1)}, bf16[2,2,80,128]{3,2,1,0:T(8,128)(2,1)S(1)}, u32[]{:S(2)}, u32[]{:S(2)}) %collective-permute-start.4) | collective-permute-done | bytes 81952 | tf_op jit(solution)/shard_map/ppermute | solution.py:408
  15.7 0.1 collective-permute-start.5
  15.8 0.6 %collective-permute-start.3 = (f32[80,256]{1,0:T(8,128)S(1)}, f32[80,256]{1,0:T(8,128)S(1)}, u32[]{:S(2)}, u32[]{:S(2)}) collective-permute-start(f32[80,256]{1,0:T(8,128)S(1)} %bitcast.10), channel_id=1, source_target_pairs={{0,1},{1,0},{2,3},{3,2},{4,5},{5,4},{6,7},{7,6},{8,9},{9,8},{10,11... | collective-permute-start | bytes 245768 | tf_op jit(solution)/shard_map/ppermute | solution.py:434
  16.4 4.2 %collective-permute-done.3.refs_1_ = f32[80,256]{1,0:T(8,128)S(1)} collective-permute-done((f32[80,256]{1,0:T(8,128)S(1)}, f32[80,256]{1,0:T(8,128)S(1)}, u32[]{:S(2)}, u32[]{:S(2)}) %collective-permute-start.3) | collective-permute-done | bytes 81952 | tf_op jit(solution)/shard_map/ppermute | solution.py:434
  20.7 0.0 collective-permute-done.5.refs_6_
  20.7 0.4 %final.1 = (bf16[2,1,80,128]{3,2,1,0:T(8,128)(2,1)S(1)}, f32[32,128]{1,0:T(8,128)S(1)}) custom-call(s32[1]{0:T(128)} %bitcast.ga_ref, f32[80,256]{1,0:T(8,128)S(1)} %get-tuple-element.23.refs_0_, f32[80,256]{1,0:T(8,128)S(1)} %collective-permute-done.3.refs_1_, bf16[2,1,80,128]{3,2,1,0:T(8,128)(2,1)S(1)} %copy-done, s32[160,128]{1,0:T(8,128)S(1)} %copy-done.1, ...), custom_call_target="tpu_custom_call" | custom-call | tf_op jit(solution)/shard_map/final/pallas_call | solution.py:464
  21.1 8.9 %all_to_all.11 = f32[32,1,128]{2,1,0:T(1,128)S(1)} all-to-all(f32[32,1,128]{2,1,0:T(1,128)S(1)} %bitcast.8), channel_id=1, replica_groups=mesh['band'=16,'ga'=2] {'ga','band'}, dimensions={0} | all-to-all | bytes 32768 | tf_op jit(solution)/shard_map/all_to_all | solution.py:472
  30.0 0.8 %assemble.1 = (bf16[2,1,80,128]{3,2,1,0:T(8,128)(2,1)}, f32[2,16,16]{2,1,0:T(8,128)}, f32[2,16,16]{2,1,0:T(8,128)}) custom-call(f32[32,128]{1,0:T(8,128)S(1)} %bitcast.7, bf16[2,1,80,128]{3,2,1,0:T(8,128)(2,1)S(1)} %get-tuple-element.30.applied_ref), custom_call_target="tpu_custom_call" | custom-call | tf_op jit(solution)/shard_map/assemble/pallas_call | solution.py:475
  (16 shorter events, 0.1 us)
Async XLA Ops:
  0.6 10.5 %collective-permute-start.1 = (bf16[2,1,80,128]{3,2,1,0:T(8,128)(2,1)}, bf16[2,1,80,128]{3,2,1,0:T(8,128)(2,1)S(1)}, u32[]{:S(2)}, u32[]{:S(2)}) collective-permute-start(bf16[2,1,80,128]{3,2,1,0:T(8,128)(2,1)} %refs_2_.1), channel_id=1, source_target_pairs={{24,0},{26,2},{28,4},{30,6},{0,8},{2,10},{4,12},{6,14},{8,16},{10,... | collective-permute-start | bytes 122888 | tf_op jit(solution)/shard_map/ppermute | solution.py:383
  3.7 8.0 %collective-permute-start = (bf16[2,1,80,128]{3,2,1,0:T(8,128)(2,1)}, bf16[2,1,80,128]{3,2,1,0:T(8,128)(2,1)S(1)}, u32[]{:S(2)}, u32[]{:S(2)}) collective-permute-start(bf16[2,1,80,128]{3,2,1,0:T(8,128)(2,1)} %refs_2_.1), channel_id=1, source_target_pairs={{0,1},{1,0},{2,3},{3,2},{4,5},{5,4},{6,7},{7,6},{8,9},{9,8},{10,11... | collective-permute-start | bytes 122888 | tf_op jit(solution)/shard_map/ppermute | solution.py:379
  5.2 8.7 %collective-permute-start.2 = (bf16[2,1,80,128]{3,2,1,0:T(8,128)(2,1)}, bf16[2,1,80,128]{3,2,1,0:T(8,128)(2,1)S(1)}, u32[]{:S(2)}, u32[]{:S(2)}) collective-permute-start(bf16[2,1,80,128]{3,2,1,0:T(8,128)(2,1)} %refs_2_.1), channel_id=1, source_target_pairs={{16,0},{18,2},{20,4},{22,6},{24,8},{26,10},{28,12},{30,14},{4,16},... | collective-permute-start | bytes 122888 | tf_op jit(solution)/shard_map/ppermute | solution.py:383
  8.8 0.7 %copy-start.2 = (s32[160]{0:T(256)S(1)}, s32[160]{0:T(256)}, u32[]{:S(2)}) copy-start(s32[160]{0:T(256)} %param.10) | copy-start | bytes 1924
  8.8 0.9 %copy-start.1 = (s32[160,128]{1,0:T(8,128)S(1)}, s32[160,128]{1,0:T(8,128)}, u32[]{:S(2)}) copy-start(s32[160,128]{1,0:T(8,128)} %refs_3_.1) | copy-start | bytes 245764
  8.8 0.9 %copy-start = (bf16[2,1,80,128]{3,2,1,0:T(8,128)(2,1)S(1)}, bf16[2,1,80,128]{3,2,1,0:T(8,128)(2,1)}, u32[]{:S(2)}) copy-start(bf16[2,1,80,128]{3,2,1,0:T(8,128)(2,1)} %refs_2_.1) | copy-start | bytes 122884
  9.7 2.1 %copy-start.3 = (f32[240,480]{1,0:T(8,128)S(1)}, f32[240,480]{1,0:T(8,128)}, u32[]{:S(2)}) copy-start(f32[240,480]{1,0:T(8,128)} %refs_5_.1) | copy-start | bytes 1382404
  9.7 2.1 %copy-start.4 = (bf16[2,2,256,240]{3,2,1,0:T(8,128)(2,1)S(1)}, bf16[2,2,256,240]{3,2,1,0:T(8,128)(2,1)}, u32[]{:S(2)}) copy-start(bf16[2,2,256,240]{3,2,1,0:T(8,128)(2,1)} %constant.13.clone.refs_7_) | copy-start | bytes 1474564
  9.7 2.1 %copy-start.5 = (bf16[2,480,256]{2,1,0:T(8,128)(2,1)S(1)}, bf16[2,480,256]{2,1,0:T(8,128)(2,1)}, u32[]{:S(2)}) copy-start(bf16[2,480,256]{2,1,0:T(8,128)(2,1)} %constant.12.clone.refs_6_) | copy-start | bytes 1474564
  9.7 2.1 %copy-start.6 = (bf16[2,128,480]{2,1,0:T(8,128)(2,1)S(1)}, bf16[2,128,480]{2,1,0:T(8,128)(2,1)}, u32[]{:S(2)}) copy-start(bf16[2,128,480]{2,1,0:T(8,128)(2,1)} %constant.14.clone.refs_8_) | copy-start | bytes 737284
  11.1 0.9 %copy-start.7 = (bf16[480,256]{1,0:T(8,128)(2,1)S(1)}, bf16[480,256]{1,0:T(8,128)(2,1)}, u32[]{:S(2)}) copy-start(bf16[480,256]{1,0:T(8,128)(2,1)} %constant.15.clone.refs_9_) | copy-start | bytes 737284
  11.2 4.5 %collective-permute-start.4 = (bf16[2,2,80,128]{3,2,1,0:T(8,128)(2,1)S(1)}, bf16[2,2,80,128]{3,2,1,0:T(8,128)(2,1)S(1)}, u32[]{:S(2)}, u32[]{:S(2)}) collective-permute-start(bf16[2,2,80,128]{3,2,1,0:T(8,128)(2,1)S(1)} %pad_maximum_fusion), channel_id=1, source_target_pairs={{0,4},{2,6},{4,0},{6,2},{8,12},{10,14},{12,8},{14,10},{16,20},{18,... | collective-permute-start | bytes 245768 | tf_op jit(solution)/shard_map/ppermute | solution.py:408
  15.7 4.9 %collective-permute-start.5 = (bf16[2,5,80,128]{3,2,1,0:T(8,128)(2,1)S(1)}, bf16[2,5,80,128]{3,2,1,0:T(8,128)(2,1)S(1)}, u32[]{:S(2)}, u32[]{:S(2)}) collective-permute-start(bf16[2,5,80,128]{3,2,1,0:T(8,128)(2,1)S(1)} %constant_dynamic-update-slice_fusion.refs_5_), channel_id=1, source_target_pairs={{0,2},{2,0},{4,6},{6,4},{8,10},{10,8},{12,14},{14,12},{16,18},{18,... | collective-permute-start | bytes 614408 | tf_op jit(solution)/shard_map/ppermute | solution.py:430
  15.8 4.8 %collective-permute-start.3 = (f32[80,256]{1,0:T(8,128)S(1)}, f32[80,256]{1,0:T(8,128)S(1)}, u32[]{:S(2)}, u32[]{:S(2)}) collective-permute-start(f32[80,256]{1,0:T(8,128)S(1)} %bitcast.10), channel_id=1, source_target_pairs={{0,1},{1,0},{2,3},{3,2},{4,5},{5,4},{6,7},{7,6},{8,9},{9,8},{10,11... | collective-permute-start | bytes 245768 | tf_op jit(solution)/shard_map/ppermute | solution.py:434

commit v4 on v3

--- a/solution.py
+++ b/solution.py
@@ -357,22 +357,24 @@
     sticks = slot_sticks.reshape(1, groups * slots)
     tables = [jnp.asarray(t) for t in twiddle_tables(points, radius, groups)]
 
-    rows = pl.pallas_call(
+    set_rows = pl.pallas_call(
         rows_kernel,
         out_shape=jax.ShapeDtypeStruct((width, 128), F32),
         out_specs=VMEM_SPEC,
         compiler_params=KERNEL_PARAMS,
         cost_estimate=pl.CostEstimate(flops=FIRST_FLOPS, bytes_accessed=0, transcendentals=0),
         name="rows",
-    )()
-    sticks = pl.pallas_call(
+    )
+    copy_sticks = pl.pallas_call(
         copy_kernel,
         out_shape=jax.ShapeDtypeStruct(sticks.shape, jnp.int32),
         in_specs=[VMEM_SPEC, VMEM_SPEC],
         out_specs=VMEM_SPEC,
         compiler_params=KERNEL_PARAMS,
         name="sticks",
-    )(rows, sticks)
+    )
+    rows = set_rows()
+    sticks = copy_sticks(rows, sticks)
     others = []
     for distance in range(1, groups):
         pairs = [(i, (i + distance) % groups) for i in range(groups)]

time: 30.9 us -> 30.9 us (level)
  no operation moved by 1% of the time
where the time goes in v4:
time: 30.9 us; the launch traced here: 30.7 us
  starting transfers between devices  9.38 us (30%)
  blocking collectives  8.87 us (29%)
  waiting for transfers between devices  5.99 us (19%)
  Pallas kernels  4.48 us (14%)
  local copies, waits for them, and re-layouts  1.23 us (4%)
  between operations  0.76 us (2%)
    all_to_all x1, blocking collectives, body(): lax.all_to_all(sums, ('ga', 'band'), split_axis=0, concat_axis=0, tiled=T...  8.87 us
    ppermute x2, starting transfers between devices, body(): lax.ppermute(orbitals, 'band', layout.pairs(part))  6.65 us
    ppermute x1, waiting for transfers between devices, body(): partials.append(lax.ppermute(send[distance - 1], 'ga', pairs))  4.25 us
    pallas_call x1, Pallas kernels, body(): grid(ga, *others, coeffs, inverse, into, pick, potential, *tables)  1.85 us
    ppermute x1, waiting for transfers between devices, body(): psi.append(lax.ppermute(near, 'band', pairs))  1.73 us
    ppermute x1, starting transfers between devices, body(): others.append(lax.ppermute(orbitals, 'ga', pairs))  1.49 us
    pallas_call x1, Pallas kernels, body(): place(ga, rows, orbitals, stick_entries, sticks)  1.43 us
    unnamed x19, local copies, waits for them, and re-layouts  1.22 us
  transfers between devices with their start and end apart: 6, of which 2 were waited for; matrix products, arithmetic and copies ran while one was open for 0% of the time, Pallas kernels for 11%

profile of v4, /device:TPU:0, one launch (start us, length us, event | category | flops | bytes accessed | tf_op | source)
XLA Modules:
  0.0 30.7 jit_solution(2606642561461650201)
XLA Ops:
  0.6 3.1 %collective-permute-start.1 = (bf16[2,1,80,128]{3,2,1,0:T(8,128)(2,1)}, bf16[2,1,80,128]{3,2,1,0:T(8,128)(2,1)S(1)}, u32[]{:S(2)}, u32[]{:S(2)}) collective-permute-start(bf16[2,1,80,128]{3,2,1,0:T(8,128)(2,1)} %refs_2_.1), channel_id=1, source_target_pairs={{24,0},{26,2},{28,4},{30,6},{0,8},{2,10},{4,12},{6,14},{8,16},{10,... | collective-permute-start | bytes 122888 | tf_op jit(solution)/shard_map/ppermute | solution.py:385
  3.7 1.5 %collective-permute-start = (bf16[2,1,80,128]{3,2,1,0:T(8,128)(2,1)}, bf16[2,1,80,128]{3,2,1,0:T(8,128)(2,1)S(1)}, u32[]{:S(2)}, u32[]{:S(2)}) collective-permute-start(bf16[2,1,80,128]{3,2,1,0:T(8,128)(2,1)} %refs_2_.1), channel_id=1, source_target_pairs={{0,1},{1,0},{2,3},{3,2},{4,5},{5,4},{6,7},{7,6},{8,9},{9,8},{10,11... | collective-permute-start | bytes 122888 | tf_op jit(solution)/shard_map/ppermute | solution.py:381
  5.2 3.5 %collective-permute-start.2 = (bf16[2,1,80,128]{3,2,1,0:T(8,128)(2,1)}, bf16[2,1,80,128]{3,2,1,0:T(8,128)(2,1)S(1)}, u32[]{:S(2)}, u32[]{:S(2)}) collective-permute-start(bf16[2,1,80,128]{3,2,1,0:T(8,128)(2,1)} %refs_2_.1), channel_id=1, source_target_pairs={{16,0},{18,2},{20,4},{22,6},{24,8},{26,10},{28,12},{30,14},{4,16},... | collective-permute-start | bytes 122888 | tf_op jit(solution)/shard_map/ppermute | solution.py:385
  8.8 0.0 copy-start
  8.8 0.6 %copy-done.2 = s32[160]{0:T(256)S(1)} copy-done((s32[160]{0:T(256)S(1)}, s32[160]{0:T(256)}, u32[]{:S(2)}) %copy-start.2) | copy-done | bytes 664
  9.5 0.2 copy-done.1
  9.7 0.0 copy-done
  9.7 0.0 copy-start.6
  9.7 1.4 %place.1 = (bf16[80,256]{1,0:T(8,128)(2,1)S(1)}, s32[1,80,128]{2,1,0:T(8,128)S(1)}, bf16[2,128,80]{2,1,0:T(8,128)(2,1)S(1)}, bf16[2,80,128]{2,1,0:T(8,128)(2,1)S(1)}, f32[80,128]{1,0:T(8,128)S(1)}) custom-call(s32[1]{0:T(128)} %bitcast.ga_ref, f32[128,128]{1,0:T(8,128)S(1)} %rows.1._.rows_ref, bf16[2,1,80,128]{3,2,1,0:T(8,128)(2,1)S(1)} %copy-done, ...), custom_call_target="tpu_custom_call" | custom-call | flops 1500000000 | tf_op jit(solution)/shard_map/place/pallas_call | solution.py:404
  11.1 0.0 copy-start.7
  11.1 0.0 collective-permute-done.1
  11.2 0.6 %collective-permute-start.4 = (bf16[2,2,80,128]{3,2,1,0:T(8,128)(2,1)S(1)}, bf16[2,2,80,128]{3,2,1,0:T(8,128)(2,1)S(1)}, u32[]{:S(2)}, u32[]{:S(2)}) collective-permute-start(bf16[2,2,80,128]{3,2,1,0:T(8,128)(2,1)S(1)} %pad_maximum_fusion), channel_id=1, source_target_pairs={{0,4},{2,6},{4,0},{6,2},{8,12},{10,14},{12,8},{14,10},{16,20},{18,... | collective-permute-start | bytes 245768 | tf_op jit(solution)/shard_map/ppermute | solution.py:410
  11.8 0.0 collective-permute-done.refs_0_
  11.8 0.3 copy-done.7
  12.1 1.8 %grid.1 = (f32[80,256]{1,0:T(8,128)S(1)}, f32[1,80,256]{2,1,0:T(8,128)S(1)}) custom-call(s32[1]{0:T(128)} %bitcast.ga_ref, bf16[2,1,80,128]{3,2,1,0:T(8,128)(2,1)S(1)} %collective-permute-done.refs_0_, bf16[80,256]{1,0:T(8,128)(2,1)S(1)} %get-tuple-element.18.refs_1_, s32[1,80,128]{2,1,0:T(8,128)S(1)} %get-tuple-element.19.refs_2_, ...), custom_call_target="tpu_custom_call" | custom-call | flops 3000000000 | tf_op jit(solution)/shard_map/grid/pallas_call | solution.py:428
  13.9 0.0 collective-permute-done.2
  14.0 1.7 %collective-permute-done.4 = bf16[2,2,80,128]{3,2,1,0:T(8,128)(2,1)S(1)} collective-permute-done((bf16[2,2,80,128]{3,2,1,0:T(8,128)(2,1)S(1)}, bf16[2,2,80,128]{3,2,1,0:T(8,128)(2,1)S(1)}, u32[]{:S(2)}, u32[]{:S(2)}) %collective-permute-start.4) | collective-permute-done | bytes 81952 | tf_op jit(solution)/shard_map/ppermute | solution.py:410
  15.7 0.1 collective-permute-start.5
  15.8 0.6 %collective-permute-start.3 = (f32[80,256]{1,0:T(8,128)S(1)}, f32[80,256]{1,0:T(8,128)S(1)}, u32[]{:S(2)}, u32[]{:S(2)}) collective-permute-start(f32[80,256]{1,0:T(8,128)S(1)} %bitcast.10), channel_id=1, source_target_pairs={{0,1},{1,0},{2,3},{3,2},{4,5},{5,4},{6,7},{7,6},{8,9},{9,8},{10,11... | collective-permute-start | bytes 245768 | tf_op jit(solution)/shard_map/ppermute | solution.py:436
  16.4 4.2 %collective-permute-done.3.refs_1_ = f32[80,256]{1,0:T(8,128)S(1)} collective-permute-done((f32[80,256]{1,0:T(8,128)S(1)}, f32[80,256]{1,0:T(8,128)S(1)}, u32[]{:S(2)}, u32[]{:S(2)}) %collective-permute-start.3) | collective-permute-done | bytes 81952 | tf_op jit(solution)/shard_map/ppermute | solution.py:436
  20.7 0.0 collective-permute-done.5.refs_6_
  20.7 0.4 %final.1 = (bf16[2,1,80,128]{3,2,1,0:T(8,128)(2,1)S(1)}, f32[32,128]{1,0:T(8,128)S(1)}) custom-call(s32[1]{0:T(128)} %bitcast.ga_ref, f32[80,256]{1,0:T(8,128)S(1)} %get-tuple-element.23.refs_0_, f32[80,256]{1,0:T(8,128)S(1)} %collective-permute-done.3.refs_1_, bf16[2,1,80,128]{3,2,1,0:T(8,128)(2,1)S(1)} %copy-done, s32[160,128]{1,0:T(8,128)S(1)} %copy-done.1, ...), custom_call_target="tpu_custom_call" | custom-call | tf_op jit(solution)/shard_map/final/pallas_call | solution.py:466
  21.1 8.9 %all_to_all.11 = f32[32,1,128]{2,1,0:T(1,128)S(1)} all-to-all(f32[32,1,128]{2,1,0:T(1,128)S(1)} %bitcast.8), channel_id=1, replica_groups=mesh['band'=16,'ga'=2] {'ga','band'}, dimensions={0} | all-to-all | bytes 32768 | tf_op jit(solution)/shard_map/all_to_all | solution.py:474
  30.0 0.8 %assemble.1 = (bf16[2,1,80,128]{3,2,1,0:T(8,128)(2,1)}, f32[2,16,16]{2,1,0:T(8,128)}, f32[2,16,16]{2,1,0:T(8,128)}) custom-call(f32[32,128]{1,0:T(8,128)S(1)} %bitcast.7, bf16[2,1,80,128]{3,2,1,0:T(8,128)(2,1)S(1)} %get-tuple-element.30.applied_ref), custom_call_target="tpu_custom_call" | custom-call | tf_op jit(solution)/shard_map/assemble/pallas_call | solution.py:477
  (16 shorter events, 0.1 us)
Async XLA Ops:
  0.6 10.5 %collective-permute-start.1 = (bf16[2,1,80,128]{3,2,1,0:T(8,128)(2,1)}, bf16[2,1,80,128]{3,2,1,0:T(8,128)(2,1)S(1)}, u32[]{:S(2)}, u32[]{:S(2)}) collective-permute-start(bf16[2,1,80,128]{3,2,1,0:T(8,128)(2,1)} %refs_2_.1), channel_id=1, source_target_pairs={{24,0},{26,2},{28,4},{30,6},{0,8},{2,10},{4,12},{6,14},{8,16},{10,... | collective-permute-start | bytes 122888 | tf_op jit(solution)/shard_map/ppermute | solution.py:385
  3.7 8.0 %collective-permute-start = (bf16[2,1,80,128]{3,2,1,0:T(8,128)(2,1)}, bf16[2,1,80,128]{3,2,1,0:T(8,128)(2,1)S(1)}, u32[]{:S(2)}, u32[]{:S(2)}) collective-permute-start(bf16[2,1,80,128]{3,2,1,0:T(8,128)(2,1)} %refs_2_.1), channel_id=1, source_target_pairs={{0,1},{1,0},{2,3},{3,2},{4,5},{5,4},{6,7},{7,6},{8,9},{9,8},{10,11... | collective-permute-start | bytes 122888 | tf_op jit(solution)/shard_map/ppermute | solution.py:381
  5.2 8.7 %collective-permute-start.2 = (bf16[2,1,80,128]{3,2,1,0:T(8,128)(2,1)}, bf16[2,1,80,128]{3,2,1,0:T(8,128)(2,1)S(1)}, u32[]{:S(2)}, u32[]{:S(2)}) collective-permute-start(bf16[2,1,80,128]{3,2,1,0:T(8,128)(2,1)} %refs_2_.1), channel_id=1, source_target_pairs={{16,0},{18,2},{20,4},{22,6},{24,8},{26,10},{28,12},{30,14},{4,16},... | collective-permute-start | bytes 122888 | tf_op jit(solution)/shard_map/ppermute | solution.py:385
  8.8 0.7 %copy-start.2 = (s32[160]{0:T(256)S(1)}, s32[160]{0:T(256)}, u32[]{:S(2)}) copy-start(s32[160]{0:T(256)} %param.10) | copy-start | bytes 1924
  8.8 0.9 %copy-start.1 = (s32[160,128]{1,0:T(8,128)S(1)}, s32[160,128]{1,0:T(8,128)}, u32[]{:S(2)}) copy-start(s32[160,128]{1,0:T(8,128)} %refs_3_.1) | copy-start | bytes 245764
  8.8 0.9 %copy-start = (bf16[2,1,80,128]{3,2,1,0:T(8,128)(2,1)S(1)}, bf16[2,1,80,128]{3,2,1,0:T(8,128)(2,1)}, u32[]{:S(2)}) copy-start(bf16[2,1,80,128]{3,2,1,0:T(8,128)(2,1)} %refs_2_.1) | copy-start | bytes 122884
  9.7 2.1 %copy-start.3 = (f32[240,480]{1,0:T(8,128)S(1)}, f32[240,480]{1,0:T(8,128)}, u32[]{:S(2)}) copy-start(f32[240,480]{1,0:T(8,128)} %refs_5_.1) | copy-start | bytes 1382404
  9.7 2.1 %copy-start.4 = (bf16[2,2,256,240]{3,2,1,0:T(8,128)(2,1)S(1)}, bf16[2,2,256,240]{3,2,1,0:T(8,128)(2,1)}, u32[]{:S(2)}) copy-start(bf16[2,2,256,240]{3,2,1,0:T(8,128)(2,1)} %constant.13.clone.refs_7_) | copy-start | bytes 1474564
  9.7 2.1 %copy-start.5 = (bf16[2,480,256]{2,1,0:T(8,128)(2,1)S(1)}, bf16[2,480,256]{2,1,0:T(8,128)(2,1)}, u32[]{:S(2)}) copy-start(bf16[2,480,256]{2,1,0:T(8,128)(2,1)} %constant.12.clone.refs_6_) | copy-start | bytes 1474564
  9.7 2.1 %copy-start.6 = (bf16[2,128,480]{2,1,0:T(8,128)(2,1)S(1)}, bf16[2,128,480]{2,1,0:T(8,128)(2,1)}, u32[]{:S(2)}) copy-start(bf16[2,128,480]{2,1,0:T(8,128)(2,1)} %constant.14.clone.refs_8_) | copy-start | bytes 737284
  11.1 0.9 %copy-start.7 = (bf16[480,256]{1,0:T(8,128)(2,1)S(1)}, bf16[480,256]{1,0:T(8,128)(2,1)}, u32[]{:S(2)}) copy-start(bf16[480,256]{1,0:T(8,128)(2,1)} %constant.15.clone.refs_9_) | copy-start | bytes 737284
  11.2 4.5 %collective-permute-start.4 = (bf16[2,2,80,128]{3,2,1,0:T(8,128)(2,1)S(1)}, bf16[2,2,80,128]{3,2,1,0:T(8,128)(2,1)S(1)}, u32[]{:S(2)}, u32[]{:S(2)}) collective-permute-start(bf16[2,2,80,128]{3,2,1,0:T(8,128)(2,1)S(1)} %pad_maximum_fusion), channel_id=1, source_target_pairs={{0,4},{2,6},{4,0},{6,2},{8,12},{10,14},{12,8},{14,10},{16,20},{18,... | collective-permute-start | bytes 245768 | tf_op jit(solution)/shard_map/ppermute | solution.py:410
  15.7 4.9 %collective-permute-start.5 = (bf16[2,5,80,128]{3,2,1,0:T(8,128)(2,1)S(1)}, bf16[2,5,80,128]{3,2,1,0:T(8,128)(2,1)S(1)}, u32[]{:S(2)}, u32[]{:S(2)}) collective-permute-start(bf16[2,5,80,128]{3,2,1,0:T(8,128)(2,1)S(1)} %constant_dynamic-update-slice_fusion.refs_5_), channel_id=1, source_target_pairs={{0,2},{2,0},{4,6},{6,4},{8,10},{10,8},{12,14},{14,12},{16,18},{18,... | collective-permute-start | bytes 614408 | tf_op jit(solution)/shard_map/ppermute | solution.py:432
  15.8 4.8 %collective-permute-start.3 = (f32[80,256]{1,0:T(8,128)S(1)}, f32[80,256]{1,0:T(8,128)S(1)}, u32[]{:S(2)}, u32[]{:S(2)}) collective-permute-start(f32[80,256]{1,0:T(8,128)S(1)} %bitcast.10), channel_id=1, source_target_pairs={{0,1},{1,0},{2,3},{3,2},{4,5},{5,4},{6,7},{7,6},{8,9},{9,8},{10,11... | collective-permute-start | bytes 245768 | tf_op jit(solution)/shard_map/ppermute | solution.py:436
